TPU v7x, 512 devices: a whole 4x8x8 slice. The times are simulated.
512 devices in a mesh: region: 128 (over z_hi, y, x), member: 4 (over z_lo, core).
Axes of the slice: x: 4, y: 8, z: 8 (z_hi: 4, z_lo: 2; z = z_hi * 2 + z_lo), core: 2. Of those that a mesh axis runs over, the one named last changes fastest.
Arguments:
- ensemble: float32 [4, 1024, 8192], P('member', 'region'), may hold values from -9 to 15, as said below
- band_index: int32 [4, 1024, 8192], P('member', 'region'), may hold values from 0 to 63
- region_cells: int32 [128], P('region'), may hold values from 8192 to 65536, as said below
- target_means: float32 [128, 64], P('region'), may hold values from -8 to 8
Outputs:
- corrected: float32 [4, 1024, 8192], P('member', 'region')
Inputs may be any that keep to these rules, and one draw needn't show every extreme that they name: `ensemble`: finite values. `region_cells`: at least one eighth of a tile; one region in every draw holds its whole tile.
All inputs are finite; a program needn't handle non-finite values.
Results may differ from a plain program's by a relative error of at most 0.000057.
Values sent between devices are 32-bit elements; how exact they have to be, the bound alone decides.
No kernel may reach another device: no remote copies, remote signals or barrier semaphores. Data moves between devices by JAX's collectives and lax.ppermute only.
A program may use at most 64 MiB of HBM per device.

v0:
```python
import jax
import jax.numpy as jnp
from jax import lax
from jax.sharding import PartitionSpec as P


def extended_2(shard, sides, width):
    for axis, dim in sides:
        devices, length = (lax.axis_size(axis), shard.shape[dim])
        up = [(i, (i + 1) % devices) for i in range(devices - 1)]
        down = [(j, i) for i, j in up]
        last = lax.slice_in_dim(shard, length - width, length, axis=dim)
        leading = lax.slice_in_dim(shard, 0, width, axis=dim)
        before = lax.ppermute(last, axis, up)
        after = lax.ppermute(leading, axis, down)
        shard = jnp.concatenate([before, shard, after], axis=dim)
    return shard


def total_of_pieces(shard, axis):
    pieces = lax.all_gather(shard, axis)
    return pieces.sum(axis=0)


def smooth_pass(extended):
    vertical = extended[:, :-2] + 2.0 * extended[:, 1:-1] + extended[:, 2:]
    across = jnp.roll(vertical, 1, axis=2) + 2.0 * vertical + jnp.roll(vertical, -1, axis=2)
    return across / 16.0


def pole_fix(extended, layers, at_north, at_south):
    total = extended.shape[1]
    row_ids = jnp.arange(total, dtype=jnp.int32)[None, :, None]
    north_row = extended[:, layers : layers + 1]
    south_row = extended[:, total - layers - 1 : total - layers]
    extended = jnp.where(jnp.logical_and(at_north, row_ids < layers), north_row, extended)
    return jnp.where(jnp.logical_and(at_south, row_ids >= total - layers), south_row, extended)


def shards(ensemble, band_index, region_cells, target_means):
    region_count = lax.axis_size("region")
    region_rank = lax.axis_index("region")
    at_north = region_rank == 0
    at_south = region_rank == region_count - 1
    extended = extended_2(ensemble, (("region", 1),), 2)
    extended = pole_fix(extended, 2, at_north, at_south)
    middle = pole_fix(smooth_pass(extended), 1, at_north, at_south)
    smoothed = smooth_pass(middle)
    members, lat_rows, lon_cells = smoothed.shape
    bands_total = target_means.shape[1]
    position = (
        jnp.arange(lat_rows, dtype=jnp.int32)[:, None] * lon_cells
        + jnp.arange(lon_cells, dtype=jnp.int32)[None, :]
    )
    valid_mask = (position < region_cells[0]).astype(jnp.float32)
    live_field = valid_mask[None]
    flat_values = smoothed.reshape(-1)
    flat_bands = band_index.reshape(-1)
    flat_live = live_field.reshape(-1)
    weighted = jnp.stack([flat_values * flat_live, flat_live])
    group_size = 8
    pieces = []
    for group in range(bands_total // group_size):
        group_ids = group * group_size + jnp.arange(group_size, dtype=jnp.int32)
        one_hot = (flat_bands[None, :] == group_ids[:, None]).astype(jnp.float32)
        pieces.append(jnp.einsum("kc,bc->kb", weighted, one_hot, precision=lax.Precision.HIGHEST))
    partial_stats = jnp.concatenate(pieces, axis=1)
    totals = total_of_pieces(partial_stats, "member")
    bordered = extended_2(totals[None], (("region", 0),), 1)
    pooled = bordered[0] + bordered[1] + bordered[2]
    offset = target_means[0] - pooled[0] / (pooled[1] + 1.0)
    applied = jnp.zeros(smoothed.shape, jnp.float32)
    for band in range(bands_total):
        applied = jnp.where(band_index == band, offset[band], applied)
    return smoothed + live_field * applied


def solution(mesh):
    placed = (
        P("member", "region", None),
        P("member", "region", None),
        P("region"),
        P("region", None),
    )
    return jax.shard_map(
        shards, mesh=mesh, in_specs=placed, out_specs=P("member", "region", None), check_vma=False
    )
```

profile of v0, /device:TPU:190, one launch (start us, length us, event | category | flops | bytes accessed | tf_op | source)
XLA Modules:
  0.0 107.8 jit_solution(11514983534822845099)
XLA Ops:
  0.0 1.1 fusion.44
  1.1 6.4 %collective-permute-start = (f32[1,2,8192]{2,1,0:T(2,128)S(1)}, f32[1,2,8192]{2,1,0:T(2,128)S(1)}, u32[]{:S(2)}, u32[]{:S(2)}) collective-permute-start(f32[1,2,8192]{2,1,0:T(2,128)S(1)} %get-tuple-element.17), channel_id=1, source_target_pairs={{0,4},{4,8},{8,12},{12,16},{16,20},{20,24},{24,28},{28,32},{32,36}... | collective-permute-start | bytes 196616 | tf_op jit(solution)/shard_map/ppermute | solution.py:14
  7.5 1.9 %collective-permute-start.1 = (f32[1,2,8192]{2,1,0:T(2,128)S(1)}, f32[1,2,8192]{2,1,0:T(2,128)S(1)}, u32[]{:S(2)}, u32[]{:S(2)}) collective-permute-start(f32[1,2,8192]{2,1,0:T(2,128)S(1)} %get-tuple-element.18), channel_id=1, source_target_pairs={{4,0},{8,4},{12,8},{16,12},{20,16},{24,20},{28,24},{32,28},{36,32}... | collective-permute-start | bytes 196616 | tf_op jit(solution)/shard_map/ppermute | solution.py:15
  9.4 1.1 %fusion.43 = (f32[1,1,8192]{2,1,0:T(1,128)S(1)}, f32[1,1,8192]{2,1,0:T(1,128)S(1)}) fusion(f32[1,8,8192]{2,1,0:T(8,128)} %param.4), kind=kLoop, calls=%fused_computation.72 | loop fusion | bytes 131072 | tf_op jit(solution)/shard_map/slice | solution.py:35
  11.4 0.2 copy.5
  11.7 0.3 convert_element_type.21
  12.1 8.4 %collective-permute-done.1 = f32[1,2,8192]{2,1,0:T(2,128)S(1)} collective-permute-done((f32[1,2,8192]{2,1,0:T(2,128)S(1)}, f32[1,2,8192]{2,1,0:T(2,128)S(1)}, u32[]{:S(2)}, u32[]{:S(2)}) %collective-permute-start.1) | collective-permute-done | bytes 65568 | tf_op jit(solution)/shard_map/ppermute | solution.py:15
  20.4 0.1 fusion.31
  20.6 0.1 slice_add_fusion
  20.7 0.2 fusion.39
  21.0 0.3 fusion.33
  21.5 0.1 fusion.41
  21.7 0.1 fusion.36
  21.9 0.3 copy.6
  22.1 0.4 broadcast_select_fusion
  22.6 2.7 %fusion = f32[2,8]{1,0:T(2,128)S(1)} fusion(s32[65536]{0:T(1024)S(1)} %bitcast.92, f32[1,65536]{1,0:T(1,128)S(1)} %convert_element_type.21, f32[1,65536]{1,0:T(1,128)S(1)} %broadcast_select_fusion), kind=kOutput, calls=%fused_computation.1 | convolution fusion | flops 13238272 | bytes 786496 | tf_op jit(solution)/shard_map/kc,bc->kb/dot_general | solution.py:66
  25.2 2.6 %fusion.1 = f32[2,8]{1,0:T(2,128)S(1)} fusion(s32[65536]{0:T(1024)S(1)} %bitcast.93, s32[8]{0:T(128)S(1)} %iota_add_fusion, f32[1,65536]{1,0:T(1,128)S(1)} %convert_element_type.21, f32[1,65536]{1,0:T(1,128)S(1)} %broadcast_select_fusion), kind=kOutput, calls=%fused_computation.2 | convolution fusion | flops 13238272 | bytes 786528 | tf_op jit(solution)/shard_map/kc,bc->kb/dot_general | solution.py:66
  27.8 2.6 %fusion.3 = f32[2,8]{1,0:T(2,128)S(1)} fusion(s32[65536]{0:T(1024)S(1)} %bitcast.94, s32[8]{0:T(128)S(1)} %iota_add_fusion.1, f32[1,65536]{1,0:T(1,128)S(1)} %convert_element_type.21, f32[1,65536]{1,0:T(1,128)S(1)} %broadcast_select_fusion), kind=kOutput, calls=%fused_computation.4 | convolution fusion | flops 13238272 | bytes 786528 | tf_op jit(solution)/shard_map/kc,bc->kb/dot_general | solution.py:66
  30.4 2.6 %fusion.5 = f32[2,8]{1,0:T(2,128)S(1)} fusion(s32[65536]{0:T(1024)S(1)} %bitcast.95, s32[8]{0:T(128)S(1)} %iota_add_fusion.2, f32[1,65536]{1,0:T(1,128)S(1)} %convert_element_type.21, f32[1,65536]{1,0:T(1,128)S(1)} %broadcast_select_fusion), kind=kOutput, calls=%fused_computation.6 | convolution fusion | flops 13238272 | bytes 786528 | tf_op jit(solution)/shard_map/kc,bc->kb/dot_general | solution.py:66
  33.0 2.6 %fusion.7 = f32[2,8]{1,0:T(2,128)S(1)} fusion(s32[65536]{0:T(1024)S(1)} %bitcast.96, s32[8]{0:T(128)S(1)} %iota_add_fusion.3, f32[1,65536]{1,0:T(1,128)S(1)} %convert_element_type.21, f32[1,65536]{1,0:T(1,128)S(1)} %broadcast_select_fusion), kind=kOutput, calls=%fused_computation.8 | convolution fusion | flops 13238272 | bytes 786528 | tf_op jit(solution)/shard_map/kc,bc->kb/dot_general | solution.py:66
  35.6 2.8 %fusion.9 = f32[2,8]{1,0:T(2,128)S(1)} fusion(s32[65536]{0:T(1024)S(1)} %bitcast.97, s32[8]{0:T(128)S(1)} %iota_add_fusion.4, f32[1,65536]{1,0:T(1,128)S(1)} %convert_element_type.21, f32[1,65536]{1,0:T(1,128)S(1)} %broadcast_select_fusion), kind=kOutput, calls=%fused_computation.10 | convolution fusion | flops 13238272 | bytes 786528 | tf_op jit(solution)/shard_map/kc,bc->kb/dot_general | solution.py:66
  38.3 2.6 %fusion.11 = f32[2,8]{1,0:T(2,128)S(1)} fusion(s32[65536]{0:T(1024)S(1)} %bitcast.98, s32[8]{0:T(128)S(1)} %iota_add_fusion.5, f32[1,65536]{1,0:T(1,128)S(1)} %convert_element_type.21, f32[1,65536]{1,0:T(1,128)S(1)} %broadcast_select_fusion), kind=kOutput, calls=%fused_computation.12 | convolution fusion | flops 13238272 | bytes 786528 | tf_op jit(solution)/shard_map/kc,bc->kb/dot_general | solution.py:66
  40.9 2.6 %fusion.13 = f32[2,8]{1,0:T(2,128)S(1)} fusion(s32[65536]{0:T(1024)S(1)} %bitcast.99, s32[8]{0:T(128)S(1)} %iota_add_fusion.6, f32[1,65536]{1,0:T(1,128)S(1)} %convert_element_type.21, f32[1,65536]{1,0:T(1,128)S(1)} %broadcast_select_fusion), kind=kOutput, calls=%fused_computation.14 | convolution fusion | flops 13238272 | bytes 786528 | tf_op jit(solution)/shard_map/kc,bc->kb/dot_general | solution.py:66
  43.6 5.1 %all-gather.1 = f32[4,2,64]{2,1,0:T(2,128)S(1)} all-gather(f32[1,2,64]{2,1,0:T(2,128)S(1)} %bitcast.104), channel_id=2, replica_groups=mesh['region'=128,'member'=4] {'member'}, dimensions={0}, use_global_device_ids=true | all-gather | bytes 2560 | tf_op jit(solution)/shard_map/all_gather | solution.py:21
  48.7 2.4 %collective-permute-start.2 = (f32[1,2,64]{2,1,0:T(2,128)S(1)}, f32[1,2,64]{2,1,0:T(2,128)S(1)}, u32[]{:S(2)}, u32[]{:S(2)}) collective-permute-start(f32[1,2,64]{2,1,0:T(2,128)S(1)} %bitcast.105), channel_id=1, source_target_pairs={{0,4},{4,8},{8,12},{12,16},{16,20},{20,24},{24,28},{28,32},{32,36}... | collective-permute-start | bytes 1544 | tf_op jit(solution)/shard_map/ppermute | solution.py:14
  51.2 3.4 %collective-permute-start.3 = (f32[1,2,64]{2,1,0:T(2,128)S(1)}, f32[1,2,64]{2,1,0:T(2,128)S(1)}, u32[]{:S(2)}, u32[]{:S(2)}) collective-permute-start(f32[1,2,64]{2,1,0:T(2,128)S(1)} %bitcast.106), channel_id=1, source_target_pairs={{4,0},{8,4},{12,8},{16,12},{20,16},{24,20},{28,24},{32,28},{36,32}... | collective-permute-start | bytes 1544 | tf_op jit(solution)/shard_map/ppermute | solution.py:15
  54.6 8.4 %collective-permute-done.3 = f32[1,2,64]{2,1,0:T(2,128)S(1)} collective-permute-done((f32[1,2,64]{2,1,0:T(2,128)S(1)}, f32[1,2,64]{2,1,0:T(2,128)S(1)}, u32[]{:S(2)}, u32[]{:S(2)}) %collective-permute-start.3) | collective-permute-done | bytes 544 | tf_op jit(solution)/shard_map/ppermute | solution.py:15
  63.0 0.7 fusion.46
  63.7 0.7 fusion.47
  64.4 0.7 fusion.45
  65.2 0.7 fusion.48
  65.8 42.0 %select_add_fusion = f32[1,8,8192]{2,1,0:T(8,128)} fusion(f32[1,8,8192]{2,1,0:T(8,128)S(1)} %fusion.36, s32[1,8,8192]{2,1,0:T(8,128)S(1)} %copy-done, f32[]{:T(128)} %bitcast.72, f32[]{:T(128)} %bitcast.71, f32[]{:T(128)} %bitcast.70, f32[]{:T(128)} %bitcast.69, f32[]{:T(128)} %bitcast.68, f32[]{:T(128)} %bitcast.67, f32[]{:T(128)} %bitcast.66, f32[]{:T(128)} %bitcast.65, ...), kind=kLoop, calls=%fused_computation.47 | loop fusion | flops 8650752 | bytes 786724 | tf_op jit(solution)/shard_map/add | solution.py:75
  (29 shorter events, 0.8 us)
Async XLA Ops:
  1.1 11.0 %collective-permute-start = (f32[1,2,8192]{2,1,0:T(2,128)S(1)}, f32[1,2,8192]{2,1,0:T(2,128)S(1)}, u32[]{:S(2)}, u32[]{:S(2)}) collective-permute-start(f32[1,2,8192]{2,1,0:T(2,128)S(1)} %get-tuple-element.17), channel_id=1, source_target_pairs={{0,4},{4,8},{8,12},{12,16},{16,20},{20,24},{24,28},{28,32},{32,36}... | collective-permute-start | bytes 196616 | tf_op jit(solution)/shard_map/ppermute | solution.py:14
  7.5 12.9 %collective-permute-start.1 = (f32[1,2,8192]{2,1,0:T(2,128)S(1)}, f32[1,2,8192]{2,1,0:T(2,128)S(1)}, u32[]{:S(2)}, u32[]{:S(2)}) collective-permute-start(f32[1,2,8192]{2,1,0:T(2,128)S(1)} %get-tuple-element.18), channel_id=1, source_target_pairs={{4,0},{8,4},{12,8},{16,12},{20,16},{24,20},{28,24},{32,28},{36,32}... | collective-permute-start | bytes 196616 | tf_op jit(solution)/shard_map/ppermute | solution.py:15
  9.4 2.6 %copy-start = (s32[1,8,8192]{2,1,0:T(8,128)S(1)}, s32[1,8,8192]{2,1,0:T(8,128)}, u32[]{:S(2)}) copy-start(s32[1,8,8192]{2,1,0:T(8,128)} %param.5) | copy-start | bytes 786436
  11.7 8.7 %copy-start.1 = (f32[1,8,8192]{2,1,0:T(8,128)S(1)}, f32[1,8,8192]{2,1,0:T(8,128)}, u32[]{:S(2)}) copy-start(f32[1,8,8192]{2,1,0:T(8,128)} %param.4) | copy-start | bytes 786436
  40.9 22.0 %copy-start.2 = (f32[1,64]{1,0:T(1,128)S(1)}, f32[1,64]{1,0:T(1,128)}, u32[]{:S(2)}) copy-start(f32[1,64]{1,0:T(1,128)} %param.7) | copy-start | bytes 772
  48.7 5.8 %collective-permute-start.2 = (f32[1,2,64]{2,1,0:T(2,128)S(1)}, f32[1,2,64]{2,1,0:T(2,128)S(1)}, u32[]{:S(2)}, u32[]{:S(2)}) collective-permute-start(f32[1,2,64]{2,1,0:T(2,128)S(1)} %bitcast.105), channel_id=1, source_target_pairs={{0,4},{4,8},{8,12},{12,16},{16,20},{20,24},{24,28},{28,32},{32,36}... | collective-permute-start | bytes 1544 | tf_op jit(solution)/shard_map/ppermute | solution.py:14
  51.2 11.8 %collective-permute-start.3 = (f32[1,2,64]{2,1,0:T(2,128)S(1)}, f32[1,2,64]{2,1,0:T(2,128)S(1)}, u32[]{:S(2)}, u32[]{:S(2)}) collective-permute-start(f32[1,2,64]{2,1,0:T(2,128)S(1)} %bitcast.106), channel_id=1, source_target_pairs={{4,0},{8,4},{12,8},{16,12},{20,16},{24,20},{28,24},{32,28},{36,32}... | collective-permute-start | bytes 1544 | tf_op jit(solution)/shard_map/ppermute | solution.py:15
where the time goes:
time: 109 us; the launch traced here: 108 us
  other arithmetic  43.7 us (40%)
  matrix products  20.9 us (19%)
  waiting for transfers between devices  16.8 us (15%)
  starting transfers between devices  14.2 us (13%)
  local copies, waits for them, and re-layouts  6.26 us (6%)
  blocking collectives  5.06 us (5%)
    add x1, other arithmetic, shards(): return smoothed + live_field * applied  42 us
    dot_general x8, matrix products, shards(): jnp.einsum('kc,bc->kb', weighted, one_hot, precision=lax.Precision.HIGHEST)  20.9 us
    ppermute x2, waiting for transfers between devices, extended_2(): after = lax.ppermute(leading, axis, down)  16.8 us
    ppermute x2, starting transfers between devices, extended_2(): before = lax.ppermute(last, axis, up)  8.86 us
    ppermute x2, starting transfers between devices, extended_2(): after = lax.ppermute(leading, axis, down)  5.31 us
    all_gather x1, blocking collectives, total_of_pieces(): pieces = lax.all_gather(shard, axis)  5.06 us
    slice x4, local copies, waits for them, and re-layouts, shards(): applied = jnp.where(band_index == band, offset[band], applied)  2.84 us
  transfers between devices with their start and end apart: 4, of which 2 were waited for; matrix products, arithmetic and copies ran while one was open for 2% of the time, Pallas kernels for 0%

commit v1 on v0

v1 whole, which is shorter than its diff:
```python
import functools

import jax
import jax.numpy as jnp
from jax import lax
from jax.experimental import pallas as pl
from jax.experimental.pallas import tpu as pltpu
from jax.sharding import PartitionSpec as P

LANES = 128
LOW = 32


def smooth_rows(center, before, after, at_north, at_south):
    rows = center.shape[0]
    row = lax.broadcasted_iota(jnp.int32, center.shape, 0)
    first, last = row == 0, row == rows - 1
    north, south = center[0:1], center[rows - 1 : rows]
    above = jnp.where(at_north, north, before[1:2])
    below = jnp.where(at_south, south, after[0:1])

    def vertical(field, prior, later):
        up = jnp.where(first, prior, pltpu.roll(field, 1, 0))
        down = jnp.where(last, later, pltpu.roll(field, rows - 1, 0))
        return (up + 2.0 * field + down) * 0.25

    once = vertical(center, above, below)
    outer_above = (before[0:1] + 2.0 * above + north) * 0.25
    outer_below = (south + 2.0 * below + after[1:2]) * 0.25
    outer_above = jnp.where(at_north, once[0:1], outer_above)
    outer_below = jnp.where(at_south, once[rows - 1 : rows], outer_below)
    twice = vertical(once, outer_above, outer_below)
    width = center.shape[1]
    for _ in range(2):
        west, east = pltpu.roll(twice, 1, 1), pltpu.roll(twice, width - 1, 1)
        twice = (west + 2.0 * twice + east) * 0.25
    return twice


def live_mask(cells, shape):
    row = lax.broadcasted_iota(jnp.int32, shape, 0)
    column = lax.broadcasted_iota(jnp.int32, shape, 1)
    return row * shape[1] + column < cells


def stats_kernel(bands_total, cells_ref, place_ref, center_ref, inner_ref, outer_ref, band_ref, smoothed_ref, stats_ref):
    at_north, at_south, even = place_ref[0] != 0, place_ref[1] != 0, place_ref[2] != 0
    inner, outer = inner_ref[...], outer_ref[...]
    before, after = jnp.where(even, outer, inner), jnp.where(even, inner, outer)
    smoothed = smooth_rows(center_ref[...], before, after, at_north, at_south)
    smoothed_ref[...] = smoothed
    rows = smoothed.shape[0]
    live = live_mask(cells_ref[0], smoothed.shape)
    weighted = jnp.where(live, smoothed, 0.0)
    count = jnp.where(live, 1.0, 0.0)
    high = weighted.astype(jnp.bfloat16).astype(jnp.float32)
    rest = weighted - high
    middle = rest.astype(jnp.bfloat16).astype(jnp.float32)
    low = rest - middle
    terms = [high, middle, low, count]
    band = band_ref[...]
    upper, lower = band // LOW, band % LOW
    blocks = bands_total // LOW
    left = jnp.concatenate(
        [jnp.where(upper == a, t, 0.0) for a in range(blocks) for t in terms], axis=0
    ).astype(jnp.bfloat16)
    right = jnp.concatenate(
        [jnp.where(lower == b, 1.0, 0.0) for b in range(LOW)], axis=0
    ).astype(jnp.bfloat16)
    product = lax.dot_general(left, right, (((1,), (1,)), ((), ())), preferred_element_type=jnp.float32)
    row = lax.broadcasted_iota(jnp.int32, product.shape, 0)
    column = lax.broadcasted_iota(jnp.int32, product.shape, 1)
    kept = jnp.where(row % rows == column % rows, product, 0.0)
    spans = [jnp.sum(kept[k * rows : (k + 1) * rows], axis=0, keepdims=True) for k in range(blocks * 4)]
    total = None
    for a in range(blocks):
        for what in range(2):
            if what == 0:
                line = spans[4 * a] + (spans[4 * a + 1] + spans[4 * a + 2])
            else:
                line = spans[4 * a + 3]
            source = lax.broadcasted_iota(jnp.int32, (line.shape[1], 2 * bands_total), 0)
            target = lax.broadcasted_iota(jnp.int32, (line.shape[1], 2 * bands_total), 1)
            place = jnp.where(source // rows + (a * LOW + what * bands_total) == target, 1.0, 0.0)
            part = lax.dot_general(
                jnp.broadcast_to(line, (8, line.shape[1])), place, (((1,), (0,)), ((), ())),
                precision=lax.Precision.HIGHEST, preferred_element_type=jnp.float32,
            )
            total = part if total is None else total + part
    stats_ref[...] = total[0:1]


def apply_kernel(bands_total, cells_ref, total_ref, before_ref, after_ref, target_ref, band_ref, smoothed_ref, out_ref):
    pooled = before_ref[...] + total_ref[...] + after_ref[...]
    pooled = jnp.broadcast_to(pooled, (8, LANES))
    counts = pltpu.roll(pooled, LANES - bands_total, 1)
    target = jnp.concatenate([target_ref[...]] * (LANES // bands_total), axis=1)
    table = target - pooled / (counts + 1.0)
    cells = cells_ref[0]
    rows, width = band_ref.shape
    row = lax.broadcasted_iota(jnp.int32, (rows, LANES), 0)
    column = lax.broadcasted_iota(jnp.int32, (rows, LANES), 1)
    position = row * width + column
    for k in range(width // LANES):
        here = slice(k * LANES, (k + 1) * LANES)
        applied = jnp.take_along_axis(table, band_ref[:, here], axis=1, mode="promise_in_bounds")
        live = position + k * LANES < cells
        out_ref[:, here] = smoothed_ref[:, here] + jnp.where(live, applied, 0.0)


def shards(ensemble, band_index, region_cells, target_means):
    region_count = lax.axis_size("region")
    rank = lax.axis_index("region")
    _, rows, width = ensemble.shape
    bands_total = target_means.shape[1]
    inner_pairs = [(i, i ^ 1) for i in range(region_count)]
    outer_pairs = [(i, ((i + 1) ^ 1) - 1) for i in range(1, region_count - 1)]
    field, band = ensemble[0], band_index[0]
    even = rank % 2 == 0
    first, last = field[:2], field[rows - 2 :]
    outer = lax.ppermute(jnp.where(even, first, last), "region", outer_pairs)
    inner = lax.ppermute(jnp.where(even, last, first), "region", inner_pairs)
    places = jnp.stack([rank == 0, rank == region_count - 1, even]).astype(jnp.int32)
    smem, vmem = pl.BlockSpec(memory_space=pltpu.SMEM), pl.BlockSpec(memory_space=pltpu.VMEM)
    params = pltpu.CompilerParams(vmem_limit_bytes=16 * 2**20)
    smoothed, stats = pl.pallas_call(
        functools.partial(stats_kernel, bands_total),
        out_shape=(
            jax.ShapeDtypeStruct((rows, width), jnp.float32),
            jax.ShapeDtypeStruct((1, 2 * bands_total), jnp.float32),
        ),
        in_specs=[smem, smem, vmem, vmem, vmem, vmem],
        out_specs=(vmem, vmem),
        compiler_params=params,
        name="smooth_stats",
    )(region_cells, places, field, inner, outer, band)
    total = lax.all_gather(stats, "member").sum(axis=0)
    prior = lax.ppermute(total, "region", outer_pairs)
    later = lax.ppermute(total, "region", inner_pairs)
    out = pl.pallas_call(
        functools.partial(apply_kernel, bands_total),
        out_shape=jax.ShapeDtypeStruct((rows, width), jnp.float32),
        in_specs=[smem] + [vmem] * 6,
        out_specs=vmem,
        compiler_params=params,
        name="apply",
    )(region_cells, total, prior, later, target_means, band, smoothed)
    return out[None]


def solution(mesh):
    placed = (
        P("member", "region", None),
        P("member", "region", None),
        P("region"),
        P("region", None),
    )
    return jax.shard_map(
        shards, mesh=mesh, in_specs=placed, out_specs=P("member", "region", None), check_vma=False
    )
```

time: 109 us -> 38.7 us (0.36)
  the two profiles are of different devices: /device:TPU:190 before, /device:TPU:320 now
where the time goes in v1:
time: 38.7 us; the launch traced here: 38.5 us
  starting transfers between devices  16.3 us (42%)
  waiting for transfers between devices  10.2 us (26%)
  blocking collectives  5.07 us (13%)
  Pallas kernels  4.02 us (10%)
  other arithmetic  1.22 us (3%)
  local copies, waits for them, and re-layouts  0.96 us (2%)
  between operations  0.71 us (2%)
    ppermute x1, starting transfers between devices, shards(): outer = lax.ppermute(jnp.where(even, first, last), 'region', outer_pairs)  6.65 us
    ppermute x1, waiting for transfers between devices, shards(): prior = lax.ppermute(total, 'region', outer_pairs)  6.06 us
    ppermute x1, starting transfers between devices, shards(): prior = lax.ppermute(total, 'region', outer_pairs)  5.72 us
    all_gather x1, blocking collectives, shards(): total = lax.all_gather(stats, 'member').sum(axis=0)  5.07 us
    ppermute x1, waiting for transfers between devices, shards(): outer = lax.ppermute(jnp.where(even, first, last), 'region', outer_pairs)  4.13 us
    pallas_call x1, Pallas kernels, shards(): pl.pallas_call(functools.partial(stats_kernel, bands_total), out_shape=(j...  2.99 us
    ppermute x1, starting transfers between devices, shards(): later = lax.ppermute(total, 'region', inner_pairs)  2.05 us
    ppermute x1, starting transfers between devices, shards(): inner = lax.ppermute(jnp.where(even, last, first), 'region', inner_pairs)  1.92 us
  transfers between devices with their start and end apart: 4, of which 2 were waited for; matrix products, arithmetic and copies ran while one was open for 0% of the time, Pallas kernels for 0%

profile of v1, /device:TPU:320, one launch (start us, length us, event | category | flops | bytes accessed | tf_op | source)
XLA Modules:
  0.0 38.5 jit_solution(13929551217215066951)
XLA Ops:
  0.0 0.0 copy-start
  0.0 1.1 %select_bitcast_fusion = (f32[2,8192]{1,0:T(2,128)S(1)}, f32[2,8192]{1,0:T(2,128)S(1)}) fusion(pred[]{:T(512)} %eq.13, f32[1,8,8192]{2,1,0:T(8,128)} %param.4), kind=kLoop, calls=%fused_computation | loop fusion | flops 32768 | bytes 262145 | tf_op jit(solution)/shard_map/jit(_where)/select_n | solution.py:121
  1.1 6.7 %collective-permute-start.1 = (f32[2,8192]{1,0:T(2,128)S(1)}, f32[2,8192]{1,0:T(2,128)S(1)}, u32[]{:S(2)}, u32[]{:S(2)}) collective-permute-start(f32[2,8192]{1,0:T(2,128)S(1)} %get-tuple-element.9), channel_id=1, source_target_pairs={{4,8},{8,4},{12,16},{16,12},{20,24},{24,20},{28,32},{32,28},{36,40... | collective-permute-start | bytes 196616 | tf_op jit(solution)/shard_map/ppermute | solution.py:121
  7.8 1.9 %collective-permute-start = (f32[2,8192]{1,0:T(2,128)S(1)}, f32[2,8192]{1,0:T(2,128)S(1)}, u32[]{:S(2)}, u32[]{:S(2)}) collective-permute-start(f32[2,8192]{1,0:T(2,128)S(1)} %get-tuple-element.10), channel_id=1, source_target_pairs={{0,4},{4,0},{8,12},{12,8},{16,20},{20,16},{24,28},{28,24},{32,36},... | collective-permute-start | bytes 196616 | tf_op jit(solution)/shard_map/ppermute | solution.py:122
  10.4 0.1 add_convert_fusion.place_ref
  10.4 4.1 %collective-permute-done.1.outer_ref = f32[2,8192]{1,0:T(2,128)S(1)} collective-permute-done((f32[2,8192]{1,0:T(2,128)S(1)}, f32[2,8192]{1,0:T(2,128)S(1)}, u32[]{:S(2)}, u32[]{:S(2)}) %collective-permute-start.1) | collective-permute-done | bytes 65568 | tf_op jit(solution)/shard_map/ppermute | solution.py:121
  14.6 0.0 collective-permute-done.inner_ref
  14.6 0.0 copy-done
  14.6 0.0 copy-start.1
  14.6 0.9 %copy-done.1 = f32[1,8,8192]{2,1,0:T(8,128)S(1)} copy-done((f32[1,8,8192]{2,1,0:T(8,128)S(1)}, f32[1,8,8192]{2,1,0:T(8,128)}, u32[]{:S(2)}) %copy-start.1) | copy-done | bytes 262168
  15.5 3.0 %smooth_stats.1 = (f32[8,8192]{1,0:T(8,128)S(1)}, f32[1,128]{1,0:T(1,128)S(1)}) custom-call(s32[1]{0:T(128)S(6)} %copy.5.cells_ref, s32[3]{0:T(128)S(1)} %add_convert_fusion.place_ref, f32[8,8192]{1,0:T(8,128)S(1)} %bitcast.14, f32[2,8192]{1,0:T(2,128)S(1)} %collective-permute-done.inner_ref, f32[2,8192]{1,0:T(2,128)S(1)} %collective-permute-done.1.outer_ref, ...), custom_call_target="tpu_custom_call" | custom-call | tf_op jit(solution)/shard_map/smooth_stats/pallas_call | solution.py:126
  18.5 5.1 %all-gather.1 = f32[4,1,128]{2,1,0:T(1,128)S(1)} all-gather(f32[1,1,128]{2,1,0:T(1,128)S(1)} %bitcast.18), channel_id=2, replica_groups=mesh['region'=128,'member'=4] {'member'}, dimensions={0}, use_global_device_ids=true | all-gather | bytes 2560 | tf_op jit(solution)/shard_map/all_gather | solution.py:137
  23.6 0.0 copy-start.2
  23.6 2.1 %collective-permute-start.3 = (f32[1,128]{1,0:T(1,128)S(1)}, f32[1,128]{1,0:T(1,128)S(1)}, u32[]{:S(2)}, u32[]{:S(2)}) collective-permute-start(f32[1,128]{1,0:T(1,128)S(1)} %bitcast.15), channel_id=1, source_target_pairs={{0,4},{4,0},{8,12},{12,8},{16,20},{20,16},{24,28},{28,24},{32,36},... | collective-permute-start | bytes 1544 | tf_op jit(solution)/shard_map/ppermute | solution.py:139
  25.7 5.7 %collective-permute-start.2 = (f32[1,128]{1,0:T(1,128)S(1)}, f32[1,128]{1,0:T(1,128)S(1)}, u32[]{:S(2)}, u32[]{:S(2)}) collective-permute-start(f32[1,128]{1,0:T(1,128)S(1)} %bitcast.16), channel_id=1, source_target_pairs={{4,8},{8,4},{12,16},{16,12},{20,24},{24,20},{28,32},{32,28},{36,40... | collective-permute-start | bytes 1544 | tf_op jit(solution)/shard_map/ppermute | solution.py:138
  31.4 0.0 collective-permute-done.3.after_ref
  31.4 6.1 %collective-permute-done.2.before_ref = f32[1,128]{1,0:T(1,128)S(1)} collective-permute-done((f32[1,128]{1,0:T(1,128)S(1)}, f32[1,128]{1,0:T(1,128)S(1)}, u32[]{:S(2)}, u32[]{:S(2)}) %collective-permute-start.2) | collective-permute-done | bytes 544 | tf_op jit(solution)/shard_map/ppermute | solution.py:138
  37.5 0.0 copy-done.2
  37.5 1.0 %apply.1 = f32[8,8192]{1,0:T(8,128)} custom-call(s32[1]{0:T(128)S(6)} %copy.5.cells_ref, f32[1,128]{1,0:T(1,128)S(1)} %bitcast.17, f32[1,128]{1,0:T(1,128)S(1)} %collective-permute-done.2.before_ref, f32[1,128]{1,0:T(1,128)S(1)} %collective-permute-done.3.after_ref, f32[1,64]{1,0:T(1,128)S(1)} %copy-done.2, s32[8,8192]{1,0:T(8,128)S(1)} %bitcast.13, ...), custom_call_target="tpu_custom_call" | custom-call | tf_op jit(solution)/shard_map/apply/pallas_call | solution.py:140
  (1 shorter events, 0.0 us)
Async XLA Ops:
  0.0 14.6 %copy-start = (s32[1,8,8192]{2,1,0:T(8,128)S(1)}, s32[1,8,8192]{2,1,0:T(8,128)}, u32[]{:S(2)}) copy-start(s32[1,8,8192]{2,1,0:T(8,128)} %param.5) | copy-start | bytes 786436
  1.1 13.4 %collective-permute-start.1 = (f32[2,8192]{1,0:T(2,128)S(1)}, f32[2,8192]{1,0:T(2,128)S(1)}, u32[]{:S(2)}, u32[]{:S(2)}) collective-permute-start(f32[2,8192]{1,0:T(2,128)S(1)} %get-tuple-element.9), channel_id=1, source_target_pairs={{4,8},{8,4},{12,16},{16,12},{20,24},{24,20},{28,32},{32,28},{36,40... | collective-permute-start | bytes 196616 | tf_op jit(solution)/shard_map/ppermute | solution.py:121
  7.8 6.8 %collective-permute-start = (f32[2,8192]{1,0:T(2,128)S(1)}, f32[2,8192]{1,0:T(2,128)S(1)}, u32[]{:S(2)}, u32[]{:S(2)}) collective-permute-start(f32[2,8192]{1,0:T(2,128)S(1)} %get-tuple-element.10), channel_id=1, source_target_pairs={{0,4},{4,0},{8,12},{12,8},{16,20},{20,16},{24,28},{28,24},{32,36},... | collective-permute-start | bytes 196616 | tf_op jit(solution)/shard_map/ppermute | solution.py:122
  14.6 1.0 %copy-start.1 = (f32[1,8,8192]{2,1,0:T(8,128)S(1)}, f32[1,8,8192]{2,1,0:T(8,128)}, u32[]{:S(2)}) copy-start(f32[1,8,8192]{2,1,0:T(8,128)} %param.4) | copy-start | bytes 786436
  23.6 13.9 %copy-start.2 = (f32[1,64]{1,0:T(1,128)S(1)}, f32[1,64]{1,0:T(1,128)}, u32[]{:S(2)}) copy-start(f32[1,64]{1,0:T(1,128)} %target_ref.1) | copy-start | bytes 772
  23.6 7.8 %collective-permute-start.3 = (f32[1,128]{1,0:T(1,128)S(1)}, f32[1,128]{1,0:T(1,128)S(1)}, u32[]{:S(2)}, u32[]{:S(2)}) collective-permute-start(f32[1,128]{1,0:T(1,128)S(1)} %bitcast.15), channel_id=1, source_target_pairs={{0,4},{4,0},{8,12},{12,8},{16,20},{20,16},{24,28},{28,24},{32,36},... | collective-permute-start | bytes 1544 | tf_op jit(solution)/shard_map/ppermute | solution.py:139
  25.7 11.8 %collective-permute-start.2 = (f32[1,128]{1,0:T(1,128)S(1)}, f32[1,128]{1,0:T(1,128)S(1)}, u32[]{:S(2)}, u32[]{:S(2)}) collective-permute-start(f32[1,128]{1,0:T(1,128)S(1)} %bitcast.16), channel_id=1, source_target_pairs={{4,8},{8,4},{12,16},{16,12},{20,24},{24,20},{28,32},{32,28},{36,40... | collective-permute-start | bytes 1544 | tf_op jit(solution)/shard_map/ppermute | solution.py:138

commit v2 on v1

v2 whole, which is shorter than its diff:
```python
import functools

import jax
import jax.numpy as jnp
from jax import lax
from jax.experimental import pallas as pl
from jax.experimental.pallas import tpu as pltpu
from jax.sharding import PartitionSpec as P

LANES = 128
SUBLANES = 8
LOW = 32


def iota(shape, axis):
    return lax.broadcasted_iota(jnp.int32, shape, axis)


def west_east(field):
    half, width = SUBLANES // 2, field.shape[1]
    lane = iota(field.shape, 1)
    west, east = pltpu.roll(field, 1, 1), pltpu.roll(field, width - 1, 1)
    west = jnp.where(lane == 0, pltpu.roll(west, half, 0), west)
    east = jnp.where(lane == width - 1, pltpu.roll(east, half, 0), east)
    return west, east


def bf16_terms(values):
    high = values.astype(jnp.bfloat16).astype(jnp.float32)
    rest = values - high
    middle = rest.astype(jnp.bfloat16).astype(jnp.float32)
    return [high, middle, rest - middle]


def band_lines(bands_total, code, groups):
    blocks = bands_total // LOW
    upper, lower = code // LOW, code % LOW
    terms = [t for group in groups for t in group]
    left = jnp.concatenate(
        [jnp.where(upper == a, t, 0.0) for a in range(blocks) for t in terms], axis=0
    ).astype(jnp.bfloat16)
    right = jnp.concatenate(
        [jnp.where(lower == b, 1.0, 0.0) for b in range(LOW)], axis=0
    ).astype(jnp.bfloat16)
    product = lax.dot_general(left, right, (((1,), (1,)), ((), ())), preferred_element_type=jnp.float32)
    kept = jnp.where(iota(product.shape, 0) % SUBLANES == iota(product.shape, 1) % SUBLANES, product, 0.0)
    lines, at = [], 0
    for a in range(blocks):
        for group in groups:
            block = kept[at * SUBLANES : (at + 1) * SUBLANES]
            for k in range(1, len(group)):
                block = block + kept[(at + k) * SUBLANES : (at + k + 1) * SUBLANES]
            at += len(group)
            lines.append(jnp.sum(block, axis=0, keepdims=True))
    sublane = iota((SUBLANES, product.shape[1]), 0)
    stacked = jnp.zeros((SUBLANES, product.shape[1]), jnp.float32)
    for k, line in enumerate(lines):
        stacked = jnp.where(sublane == k, line, stacked)
    width = stacked.shape[1]
    for shift in (1, 2, 4):
        stacked = stacked + pltpu.roll(stacked, width - shift, 1)
    lane = iota((SUBLANES, LANES), 1)
    per = LANES // SUBLANES
    pick = (lane % per) * SUBLANES
    placed = None
    for k in range(width // LANES):
        part = jnp.take_along_axis(stacked[:, k * LANES : (k + 1) * LANES], pick, axis=1, mode="promise_in_bounds")
        placed = part if placed is None else jnp.where((lane % LOW) // per == k, part, placed)
    total = None
    for a in range(blocks):
        for g in range(len(groups)):
            here = (iota((SUBLANES, LANES), 0) == a * len(groups) + g) & (lane // LOW == g * blocks + a)
            part = jnp.where(here, placed, 0.0)
            total = part if total is None else total + part
    return jnp.sum(total, axis=0, keepdims=True)


def packed_edges(field):
    half = field.shape[1] // 2
    west, east = pltpu.roll(field[:, :half], 2, 0), pltpu.roll(field[:, half:], 6, 0)
    return jnp.where(iota(west.shape, 0) < SUBLANES // 2, west, east)


def prepare_kernel(bands_total, cells_ref, place_ref, center_ref, band_ref, base_ref, code_ref, stats_ref):
    at_north, at_south = place_ref[0] != 0, place_ref[1] != 0
    center, band = center_ref[...], band_ref[...]
    rows, width = center.shape
    row = iota(center.shape, 0)
    first, last = row == 0, row == rows - 1
    north, south = center[0:1], center[rows - 1 : rows]

    def vertical(field, prior, later):
        up = jnp.where(first, prior, pltpu.roll(field, 1, 0))
        down = jnp.where(last, later, pltpu.roll(field, rows - 1, 0))
        return (up + 2.0 * field + down) * 0.25

    once = vertical(center, jnp.where(at_north, north, 0.0), jnp.where(at_south, south, 0.0))
    prior = jnp.where(at_north, once[0:1], north * 0.25)
    later = jnp.where(at_south, once[rows - 1 : rows], south * 0.25)
    base = vertical(once, prior, later)
    for _ in range(2):
        base = (pltpu.roll(base, 1, 1) + 2.0 * base + pltpu.roll(base, width - 1, 1)) * 0.25
    base_ref[...] = base
    live = row * width + iota(center.shape, 1) < cells_ref[0]
    code = jnp.where(live, band, bands_total)
    code_ref[...] = packed_edges(code)
    ones = jnp.full(base.shape, 1.0, jnp.float32)
    stats_ref[...] = band_lines(bands_total, code, [bf16_terms(base), [ones]])


def edges_kernel(bands_total, place_ref, inner_ref, outer_ref, base_ref, code_ref, prepared_ref, smoothed_ref, stats_ref):
    even = place_ref[2] != 0
    rows, width = base_ref.shape
    half = width // 2
    shape = (SUBLANES, half)
    slot = iota((SUBLANES, LANES), 0) % (SUBLANES // 2)
    low = iota(shape, 0) < SUBLANES // 2

    def weights(a, b, c, d):
        table = jnp.where(slot == 0, a, jnp.where(slot == 1, b, jnp.where(slot == 2, c, d)))
        return jnp.concatenate([table * (1.0 / 16.0)] * (half // LANES), axis=1)

    after = [weights(1.0, 4.0, 0.0, 0.0), weights(0.0, 1.0, 0.0, 0.0)]
    before = [weights(0.0, 0.0, 1.0, 0.0), weights(0.0, 0.0, 4.0, 1.0)]
    added = None
    for j in range(2):
        for ref, one, other in ((inner_ref, after, before), (outer_ref, before, after)):
            line = jnp.where(low, ref[j : j + 1, :half], ref[j : j + 1, half:])
            term = line * jnp.where(even, one[j], other[j])
            added = term if added is None else added + term
    for _ in range(2):
        west, east = west_east(added)
        added = (west + 2.0 * added + east) * 0.25
    stats = band_lines(bands_total, code_ref[...], [bf16_terms(added)])
    spread = iota(stats.shape, 1) < bands_total
    stats_ref[...] = prepared_ref[...] + jnp.where(spread, stats, 0.0)
    row = iota(shape, 0)
    edge = (row < 2) | (row >= rows - 2)
    smoothed_ref[:, :half] = base_ref[:, :half] + jnp.where(edge, pltpu.roll(added, 6, 0), 0.0)
    smoothed_ref[:, half:] = base_ref[:, half:] + jnp.where(edge, pltpu.roll(added, 2, 0), 0.0)


def apply_kernel(bands_total, cells_ref, total_ref, inner_ref, outer_ref, target_ref, band_ref, smoothed_ref, out_ref):
    pooled = total_ref[...] + inner_ref[...] + outer_ref[...]
    pooled = jnp.broadcast_to(pooled, (SUBLANES, LANES))
    counts = pltpu.roll(pooled, LANES - bands_total, 1)
    target = jnp.concatenate([target_ref[...]] * (LANES // bands_total), axis=1)
    table = target - pooled / (counts + 1.0)
    cells = cells_ref[0]
    rows, width = band_ref.shape
    position = iota((rows, LANES), 0) * width + iota((rows, LANES), 1)
    for k in range(width // LANES):
        here = slice(k * LANES, (k + 1) * LANES)
        applied = jnp.take_along_axis(table, band_ref[:, here], axis=1, mode="promise_in_bounds")
        live = position + k * LANES < cells
        out_ref[:, here] = smoothed_ref[:, here] + jnp.where(live, applied, 0.0)


def shards(ensemble, band_index, region_cells, target_means):
    region_count = lax.axis_size("region")
    rank = lax.axis_index("region")
    _, rows, width = ensemble.shape
    bands_total = target_means.shape[1]
    inner_pairs = [(i, i ^ 1) for i in range(region_count)]
    outer_pairs = [(i, ((i + 1) ^ 1) - 1) for i in range(1, region_count - 1)]
    field, band = ensemble[0], band_index[0]
    even = rank % 2 == 0
    first, last = field[:2], field[rows - 2 :]
    outer = lax.ppermute(jnp.where(even, first, last), "region", outer_pairs)
    inner = lax.ppermute(jnp.where(even, last, first), "region", inner_pairs)
    places = jnp.stack([rank == 0, rank == region_count - 1, even]).astype(jnp.int32)
    smem, vmem = pl.BlockSpec(memory_space=pltpu.SMEM), pl.BlockSpec(memory_space=pltpu.VMEM)
    params = pltpu.CompilerParams(vmem_limit_bytes=16 * 2**20)
    tile = jax.ShapeDtypeStruct((rows, width), jnp.float32)
    line = jax.ShapeDtypeStruct((1, 2 * bands_total), jnp.float32)
    cost = pl.CostEstimate(flops=4 * 10**9, bytes_accessed=4 * rows * width * 4, transcendentals=0)
    base, code, prepared = pl.pallas_call(
        functools.partial(prepare_kernel, bands_total),
        out_shape=(tile, jax.ShapeDtypeStruct((rows, width // 2), jnp.int32), line),
        in_specs=[smem, smem, vmem, vmem],
        out_specs=(vmem, vmem, vmem),
        compiler_params=params,
        cost_estimate=cost,
        name="prepare",
    )(region_cells, places, field, band)
    smoothed, stats = pl.pallas_call(
        functools.partial(edges_kernel, bands_total),
        out_shape=(tile, line),
        in_specs=[smem] + [vmem] * 5,
        out_specs=(vmem, vmem),
        compiler_params=params,
        name="edges",
    )(places, inner, outer, base, code, prepared)
    total = lax.all_gather(stats, "member").sum(axis=0)
    outer_total = lax.ppermute(total, "region", outer_pairs)
    inner_total = lax.ppermute(total, "region", inner_pairs)
    out = pl.pallas_call(
        functools.partial(apply_kernel, bands_total),
        out_shape=tile,
        in_specs=[smem] + [vmem] * 6,
        out_specs=vmem,
        compiler_params=params,
        name="apply",
    )(region_cells, total, inner_total, outer_total, target_means, band, smoothed)
    return out[None]


def solution(mesh):
    placed = (
        P("member", "region", None),
        P("member", "region", None),
        P("region"),
        P("region", None),
    )
    return jax.shard_map(
        shards, mesh=mesh, in_specs=placed, out_specs=P("member", "region", None), check_vma=False
    )
```

time: 38.7 us -> 34.7 us (0.90)
  the two profiles are of different devices: /device:TPU:320 before, /device:TPU:190 now
where the time goes in v2:
time: 34.7 us; the launch traced here: 34.5 us
  starting transfers between devices  17.4 us (50%)
  Pallas kernels  5.38 us (16%)
  blocking collectives  5.3 us (15%)
  waiting for transfers between devices  3.54 us (10%)
  other arithmetic  1.22 us (4%)
  local copies, waits for them, and re-layouts  0.96 us (3%)
  between operations  0.71 us (2%)
    ppermute x1, starting transfers between devices, shards(): outer_total = lax.ppermute(total, 'region', outer_pairs)  7.13 us
    ppermute x1, starting transfers between devices, shards(): outer = lax.ppermute(jnp.where(even, first, last), 'region', outer_pairs)  6.42 us
    all_gather x1, blocking collectives, shards(): total = lax.all_gather(stats, 'member').sum(axis=0)  5.3 us
    ppermute x1, waiting for transfers between devices, shards(): outer_total = lax.ppermute(total, 'region', outer_pairs)  2.86 us
    pallas_call x1, Pallas kernels, shards(): pl.pallas_call(functools.partial(prepare_kernel, bands_total), out_shape=...  2.56 us
    ppermute x1, starting transfers between devices, shards(): inner = lax.ppermute(jnp.where(even, last, first), 'region', inner_pairs)  1.92 us
    ppermute x1, starting transfers between devices, shards(): inner_total = lax.ppermute(total, 'region', inner_pairs)  1.92 us
    pallas_call x1, Pallas kernels, shards(): pl.pallas_call(functools.partial(edges_kernel, bands_total), out_shape=(t...  1.79 us
  transfers between devices with their start and end apart: 4, of which 2 were waited for; matrix products, arithmetic and copies ran while one was open for 0% of the time, Pallas kernels for 7%

profile of v2, /device:TPU:190, one launch (start us, length us, event | category | flops | bytes accessed | tf_op | source)
XLA Modules:
  0.0 34.5 jit_solution(913725349920864428)
XLA Ops:
  0.0 0.0 copy-start
  0.0 1.1 %select_bitcast_fusion = (f32[2,8192]{1,0:T(2,128)S(1)}, f32[2,8192]{1,0:T(2,128)S(1)}) fusion(pred[]{:T(512)} %eq.13, f32[1,8,8192]{2,1,0:T(8,128)} %param.4), kind=kLoop, calls=%fused_computation | loop fusion | flops 32768 | bytes 262145 | tf_op jit(solution)/shard_map/jit(_where)/select_n | solution.py:169
  1.1 6.4 %collective-permute-start.1 = (f32[2,8192]{1,0:T(2,128)S(1)}, f32[2,8192]{1,0:T(2,128)S(1)}, u32[]{:S(2)}, u32[]{:S(2)}) collective-permute-start(f32[2,8192]{1,0:T(2,128)S(1)} %get-tuple-element.15), channel_id=1, source_target_pairs={{4,8},{8,4},{12,16},{16,12},{20,24},{24,20},{28,32},{32,28},{36,40... | collective-permute-start | bytes 196616 | tf_op jit(solution)/shard_map/ppermute | solution.py:169
  7.6 1.9 %collective-permute-start = (f32[2,8192]{1,0:T(2,128)S(1)}, f32[2,8192]{1,0:T(2,128)S(1)}, u32[]{:S(2)}, u32[]{:S(2)}) collective-permute-start(f32[2,8192]{1,0:T(2,128)S(1)} %get-tuple-element.16), channel_id=1, source_target_pairs={{0,4},{4,0},{8,12},{12,8},{16,20},{20,16},{24,28},{28,24},{32,36},... | collective-permute-start | bytes 196616 | tf_op jit(solution)/shard_map/ppermute | solution.py:170
  10.1 0.1 add_convert_fusion.place_ref
  10.2 0.0 copy-done
  10.2 0.0 copy-start.1
  10.2 1.0 %copy-done.1 = f32[1,8,8192]{2,1,0:T(8,128)S(1)} copy-done((f32[1,8,8192]{2,1,0:T(8,128)S(1)}, f32[1,8,8192]{2,1,0:T(8,128)}, u32[]{:S(2)}) %copy-start.1) | copy-done | bytes 262168
  11.2 2.6 %prepare.1 = (f32[8,8192]{1,0:T(8,128)S(1)}, s32[8,4096]{1,0:T(8,128)S(1)}, f32[1,128]{1,0:T(1,128)S(1)}) custom-call(s32[1]{0:T(128)S(6)} %copy.5.cells_ref, s32[3]{0:T(128)S(1)} %add_convert_fusion.place_ref, f32[8,8192]{1,0:T(8,128)S(1)} %bitcast.14, s32[8,8192]{1,0:T(8,128)S(1)} %bitcast.12), custom_call_target="tpu_custom_call" | custom-call | flops 4000000000 | bytes 1048576 | tf_op jit(solution)/shard_map/prepare/pallas_call | solution.py:177
  13.7 0.0 collective-permute-done.1.outer_ref
  13.7 0.0 collective-permute-done.inner_ref
  13.7 1.8 %edges.1 = (f32[8,8192]{1,0:T(8,128)S(1)}, f32[1,128]{1,0:T(1,128)S(1)}) custom-call(s32[3]{0:T(128)S(1)} %add_convert_fusion.place_ref, f32[2,8192]{1,0:T(2,128)S(1)} %collective-permute-done.inner_ref, f32[2,8192]{1,0:T(2,128)S(1)} %collective-permute-done.1.outer_ref, f32[8,8192]{1,0:T(8,128)S(1)} %get-tuple-element.10.base_ref, ...), custom_call_target="tpu_custom_call" | custom-call | tf_op jit(solution)/shard_map/edges/pallas_call | solution.py:186
  15.5 5.3 %all-gather.1 = f32[4,1,128]{2,1,0:T(1,128)S(1)} all-gather(f32[1,1,128]{2,1,0:T(1,128)S(1)} %bitcast.18), channel_id=2, replica_groups=mesh['region'=128,'member'=4] {'member'}, dimensions={0}, use_global_device_ids=true | all-gather | bytes 2560 | tf_op jit(solution)/shard_map/all_gather | solution.py:194
  20.9 0.0 copy-start.2
  20.9 7.1 %collective-permute-start.3 = (f32[1,128]{1,0:T(1,128)S(1)}, f32[1,128]{1,0:T(1,128)S(1)}, u32[]{:S(2)}, u32[]{:S(2)}) collective-permute-start(f32[1,128]{1,0:T(1,128)S(1)} %bitcast.15), channel_id=1, source_target_pairs={{4,8},{8,4},{12,16},{16,12},{20,24},{24,20},{28,32},{32,28},{36,40... | collective-permute-start | bytes 1544 | tf_op jit(solution)/shard_map/ppermute | solution.py:195
  28.0 1.9 %collective-permute-start.2 = (f32[1,128]{1,0:T(1,128)S(1)}, f32[1,128]{1,0:T(1,128)S(1)}, u32[]{:S(2)}, u32[]{:S(2)}) collective-permute-start(f32[1,128]{1,0:T(1,128)S(1)} %bitcast.16), channel_id=1, source_target_pairs={{0,4},{4,0},{8,12},{12,8},{16,20},{20,16},{24,28},{28,24},{32,36},... | collective-permute-start | bytes 1544 | tf_op jit(solution)/shard_map/ppermute | solution.py:196
  29.9 2.9 %collective-permute-done.3.outer_ref = f32[1,128]{1,0:T(1,128)S(1)} collective-permute-done((f32[1,128]{1,0:T(1,128)S(1)}, f32[1,128]{1,0:T(1,128)S(1)}, u32[]{:S(2)}, u32[]{:S(2)}) %collective-permute-start.3) | collective-permute-done | bytes 544 | tf_op jit(solution)/shard_map/ppermute | solution.py:195
  32.8 0.7 %collective-permute-done.2.inner_ref = f32[1,128]{1,0:T(1,128)S(1)} collective-permute-done((f32[1,128]{1,0:T(1,128)S(1)}, f32[1,128]{1,0:T(1,128)S(1)}, u32[]{:S(2)}, u32[]{:S(2)}) %collective-permute-start.2) | collective-permute-done | bytes 544 | tf_op jit(solution)/shard_map/ppermute | solution.py:196
  33.5 0.0 copy-done.2
  33.5 1.0 %apply.1 = f32[8,8192]{1,0:T(8,128)} custom-call(s32[1]{0:T(128)S(6)} %copy.5.cells_ref, f32[1,128]{1,0:T(1,128)S(1)} %bitcast.17, f32[1,128]{1,0:T(1,128)S(1)} %collective-permute-done.2.inner_ref, f32[1,128]{1,0:T(1,128)S(1)} %collective-permute-done.3.outer_ref, f32[1,64]{1,0:T(1,128)S(1)} %copy-done.2, s32[8,8192]{1,0:T(8,128)S(1)} %bitcast.13, ...), custom_call_target="tpu_custom_call" | custom-call | tf_op jit(solution)/shard_map/apply/pallas_call | solution.py:197
  (1 shorter events, 0.0 us)
Async XLA Ops:
  0.0 10.2 %copy-start = (s32[1,8,8192]{2,1,0:T(8,128)S(1)}, s32[1,8,8192]{2,1,0:T(8,128)}, u32[]{:S(2)}) copy-start(s32[1,8,8192]{2,1,0:T(8,128)} %param.5) | copy-start | bytes 786436
  1.1 12.6 %collective-permute-start.1 = (f32[2,8192]{1,0:T(2,128)S(1)}, f32[2,8192]{1,0:T(2,128)S(1)}, u32[]{:S(2)}, u32[]{:S(2)}) collective-permute-start(f32[2,8192]{1,0:T(2,128)S(1)} %get-tuple-element.15), channel_id=1, source_target_pairs={{4,8},{8,4},{12,16},{16,12},{20,24},{24,20},{28,32},{32,28},{36,40... | collective-permute-start | bytes 196616 | tf_op jit(solution)/shard_map/ppermute | solution.py:169
  7.6 6.2 %collective-permute-start = (f32[2,8192]{1,0:T(2,128)S(1)}, f32[2,8192]{1,0:T(2,128)S(1)}, u32[]{:S(2)}, u32[]{:S(2)}) collective-permute-start(f32[2,8192]{1,0:T(2,128)S(1)} %get-tuple-element.16), channel_id=1, source_target_pairs={{0,4},{4,0},{8,12},{12,8},{16,20},{20,16},{24,28},{28,24},{32,36},... | collective-permute-start | bytes 196616 | tf_op jit(solution)/shard_map/ppermute | solution.py:170
  10.2 1.0 %copy-start.1 = (f32[1,8,8192]{2,1,0:T(8,128)S(1)}, f32[1,8,8192]{2,1,0:T(8,128)}, u32[]{:S(2)}) copy-start(f32[1,8,8192]{2,1,0:T(8,128)} %param.4) | copy-start | bytes 786436
  20.9 12.6 %copy-start.2 = (f32[1,64]{1,0:T(1,128)S(1)}, f32[1,64]{1,0:T(1,128)}, u32[]{:S(2)}) copy-start(f32[1,64]{1,0:T(1,128)} %target_ref.1) | copy-start | bytes 772
  20.9 11.9 %collective-permute-start.3 = (f32[1,128]{1,0:T(1,128)S(1)}, f32[1,128]{1,0:T(1,128)S(1)}, u32[]{:S(2)}, u32[]{:S(2)}) collective-permute-start(f32[1,128]{1,0:T(1,128)S(1)} %bitcast.15), channel_id=1, source_target_pairs={{4,8},{8,4},{12,16},{16,12},{20,24},{24,20},{28,32},{32,28},{36,40... | collective-permute-start | bytes 1544 | tf_op jit(solution)/shard_map/ppermute | solution.py:195
  28.0 5.5 %collective-permute-start.2 = (f32[1,128]{1,0:T(1,128)S(1)}, f32[1,128]{1,0:T(1,128)S(1)}, u32[]{:S(2)}, u32[]{:S(2)}) collective-permute-start(f32[1,128]{1,0:T(1,128)S(1)} %bitcast.16), channel_id=1, source_target_pairs={{0,4},{4,0},{8,12},{12,8},{16,20},{20,16},{24,28},{28,24},{32,36},... | collective-permute-start | bytes 1544 | tf_op jit(solution)/shard_map/ppermute | solution.py:196

commit v3 on v0

v3 whole, which is shorter than its diff:
```python
import functools

import jax
import jax.numpy as jnp
from jax import lax
from jax.experimental import pallas as pl
from jax.experimental.pallas import tpu as pltpu
from jax.sharding import PartitionSpec as P

LANES = 128
SUBLANES = 8
LOW = 16


def iota(shape, axis):
    return lax.broadcasted_iota(jnp.int32, shape, axis)


def rank_flags():
    rank = lax.axis_index("region")
    return rank == 0, rank == lax.axis_size("region") - 1, rank % 2 == 0


def smooth_along(field, kept):
    width = field.shape[1]
    lane = iota(field.shape, 1)

    def shifted(values, by, edge, turn):
        moved = pltpu.roll(values, by, 1)
        return jnp.where(lane == edge, pltpu.roll(moved, turn, 0), moved) if kept else moved

    for _ in range(2):
        field = field + shifted(field, 1, 0, kept)
        field = field + shifted(field, width - 1, width - 1, SUBLANES - kept)
    return field


def bf16_terms(values):
    high = values.astype(jnp.bfloat16).astype(jnp.float32)
    rest = values - high
    middle = rest.astype(jnp.bfloat16).astype(jnp.float32)
    return [high, middle, rest - middle]


def band_blocks(bands_total, code, values, groups):
    blocks = bands_total // LOW
    upper = jnp.floor(code * (1.0 / LOW))
    lower = code - upper * LOW
    terms = bf16_terms(values)
    terms.append(jnp.full(values.shape, 1.0, jnp.float32))
    tiles = [jnp.concatenate(terms[k : k + 2], axis=0).astype(jnp.bfloat16) for k in (0, 2)]
    upper = jnp.concatenate([upper, upper], axis=0).astype(jnp.bfloat16)
    lower = jnp.concatenate([lower, lower - 1.0], axis=0).astype(jnp.bfloat16)
    zero, one = jnp.zeros((), jnp.bfloat16), jnp.ones((), jnp.bfloat16)
    left = jnp.concatenate([jnp.where(upper == a, t, zero) for a in range(blocks) for t in tiles], axis=0)
    right = jnp.concatenate([jnp.where(lower == b, one, zero) for b in range(0, LOW, 2)], axis=0)
    product = lax.dot_general(left, right, (((1,), (1,)), ((), ())), preferred_element_type=jnp.float32)
    sublane, lane = iota((SUBLANES, LANES), 0), iota((SUBLANES, LANES), 1)
    made = []
    for mask, count in groups:
        kept = sublane == lane % SUBLANES
        kept = kept if mask is None else kept & mask
        block = jnp.zeros((SUBLANES, LANES), jnp.float32)
        for a in range(blocks):
            part = [product[(4 * a + k) * SUBLANES : (4 * a + k + 1) * SUBLANES] for k in range(4)]
            sums = jnp.sum(jnp.where(kept, part[0] + (part[1] + part[2]), 0.0), axis=0, keepdims=True)
            block = jnp.where(sublane == 2 * a, sums, block)
            if count:
                counts = jnp.sum(jnp.where(kept, part[3], 0.0), axis=0, keepdims=True)
                block = jnp.where(sublane == 2 * a + 1, counts, block)
        made.append(block)
    return made


def weigh(first, second, even, table):
    slot = iota((SUBLANES, LANES), 0) % len(table[0])
    total = None
    for values, pairs in ((first, table[0]), (second, table[1])):
        weight = jnp.zeros((SUBLANES, LANES), jnp.float32)
        for s, (a, b) in enumerate(pairs):
            weight = jnp.where(slot == s, jnp.where(even, a, b) * (1.0 / 256.0), weight)
        term = values * jnp.concatenate([weight] * (values.shape[1] // LANES), axis=1)
        total = term if total is None else total + term
    return total


def load_kernel(bands_total, field_hbm, band_hbm, target_hbm, inner_ref, field_ref, band_ref, target_ref, target, sems):
    copies = [
        pltpu.make_async_copy(field_hbm, field_ref, sems.at[0]),
        pltpu.make_async_copy(band_hbm, band_ref, sems.at[1]),
        pltpu.make_async_copy(target_hbm, target, sems.at[2]),
    ]
    for copy in copies:
        copy.start()
    _, _, even = rank_flags()
    copies[0].wait()
    rows = field_ref.shape[0]
    inner_ref[...] = jnp.where(even, field_ref[rows - 2 :, :], field_ref[:2, :])
    copies[1].wait()
    copies[2].wait()
    target_ref[:, :bands_total] = target[...]
    target_ref[:, bands_total:] = target[...]


def prepare_kernel(bands_total, cells_ref, center_ref, band_ref, base_ref, code_ref, edge_code_ref, sent_ref, stats_ref):
    at_north, at_south, even = rank_flags()
    center = center_ref[...]
    rows, width = center.shape
    row = iota(center.shape, 0)
    first, last = row == 0, row == rows - 1
    north, south = center[0:1], center[rows - 1 : rows]

    def vertical(field, prior, later):
        up = jnp.where(first, prior, pltpu.roll(field, 1, 0))
        down = jnp.where(last, later, pltpu.roll(field, rows - 1, 0))
        return (up + field) + (field + down)

    once = vertical(center, jnp.where(at_north, north, 0.0), jnp.where(at_south, south, 0.0))
    prior = jnp.where(at_north, once[0:1], north)
    later = jnp.where(at_south, once[rows - 1 : rows], south)
    base = smooth_along(vertical(once, prior, later) * (1.0 / 256.0), 0)
    base_ref[...] = base
    live = row * width + iota(center.shape, 1) < cells_ref[0]
    code = jnp.where(live, band_ref[...], bands_total)
    code_ref[...] = code
    code = code.astype(jnp.float32)
    piece = width // 4
    start = jnp.where(even, 2, 0)
    packed = None
    for q in range(4):
        part = pltpu.roll(code[:, q * piece : (q + 1) * piece], start + 2 * q, 0)
        packed = part if packed is None else jnp.where(iota(part.shape, 0) // 2 == q, part, packed)
    edge_code_ref[...] = packed
    sent_ref[0:2, :] = jnp.where(even, center[:2], center[rows - 2 :])
    sent_ref[2:4, :] = jnp.where(even, code[:2], code[rows - 2 :])
    (stats_ref[...],) = band_blocks(bands_total, code, base, [(None, True)])


def inner_kernel(bands_total, got_ref, code_ref, prepared_ref, edge_ref, added_ref, sent_ref):
    _, _, even = rank_flags()
    piece = got_ref.shape[1] // 4
    quarter = iota((SUBLANES, piece), 0) // 2
    lines = []
    for j in range(2):
        line = jnp.broadcast_to(got_ref[j : j + 1, :piece], (SUBLANES, piece))
        for q in range(1, 4):
            line = jnp.where(quarter == q, got_ref[j : j + 1, q * piece : (q + 1) * piece], line)
        lines.append(line)
    added = weigh(lines[0], lines[1], even, (((1.0, 1.0), (4.0, 0.0)), ((0.0, 4.0), (1.0, 1.0))))
    added = smooth_along(added, 2)
    added_ref[...] = added
    (block,) = band_blocks(bands_total, code_ref[...], added, [(None, False)])
    block = prepared_ref[...] + block
    width = got_ref.shape[1]
    sent_ref[:, :width] = edge_ref[...]
    sent_ref[:, width : width + LANES] = block[:4]
    sent_ref[:, width + LANES :] = block[4:]


def outer_kernel(bands_total, got_ref, sent_ref, base_ref, added_ref, smoothed_ref, blocks_ref):
    at_north, at_south, even = rank_flags()
    rows, width = base_ref.shape
    half = width // 2
    shape = (SUBLANES, half)
    low = iota(shape, 0) < SUBLANES // 2
    slot = iota(shape, 0) % (SUBLANES // 2)

    def row_of(ref, j):
        return jnp.where(low, ref[j : j + 1, :half], ref[j : j + 1, half:width])

    own = slot < 2
    lines = [jnp.where(own, row_of(got_ref, j), row_of(sent_ref, j)) for j in range(2)]
    codes = [row_of(ref, j) for ref in (sent_ref, got_ref) for j in (2, 3)]
    code = jnp.where(own, jnp.where(slot == 0, codes[0], codes[1]), jnp.where(slot == 2, codes[2], codes[3]))
    table = (((1.0, 1.0), (0.0, 4.0), (1.0, 1.0), (4.0, 0.0)), ((4.0, 0.0), (1.0, 1.0), (0.0, 4.0), (1.0, 1.0)))
    added = smooth_along(weigh(lines[0], lines[1], even, table), 4)
    alone = at_north | at_south
    code = jnp.where(alone, float(bands_total), code)
    crossing = iota((SUBLANES, LANES), 0) % 4 >= 2
    own, cross = band_blocks(bands_total, code, added, [(~crossing, False), (crossing, False)])

    def block_of(ref):
        return jnp.concatenate([ref[:, width : width + LANES], ref[:, width + LANES :]], axis=0)

    own = block_of(sent_ref) + own
    cross = block_of(got_ref) + cross
    count = blocks_ref.shape[0]
    for k in range(count):
        blocks_ref[k] = own + jnp.where((k < count // 2) == even, cross, 0.0)
    piece = width // 4
    row = iota((rows, piece), 0)
    inner_start = jnp.where(even, rows - 2, 0)
    outer_start = jnp.where(even, 0, rows - 2)
    inner_row, outer_row = row // 2 == inner_start // 2, row // 2 == outer_start // 2
    for q in range(4):
        here = slice(q * piece, (q + 1) * piece)
        there = slice(q % 2 * piece, (q % 2 + 1) * piece)
        inner = pltpu.roll(added_ref[...], inner_start + (SUBLANES - 2 * q), 0)
        outer = pltpu.roll(added[:, there], outer_start + (SUBLANES - q // 2 * 4), 0)
        smoothed_ref[:, here] = base_ref[:, here] + jnp.where(inner_row, inner, jnp.where(outer_row, outer, 0.0))


def apply_kernel(bands_total, blocks_ref, target_ref, code_ref, smoothed_ref, out_ref):
    pooled = jnp.sum(blocks_ref[...], axis=0)
    for shift in (1, 2, 4):
        pooled = pooled + pltpu.roll(pooled, LANES - shift, 1)
    sublane, lane = iota(pooled.shape, 0), iota(pooled.shape, 1)
    pooled = jnp.take_along_axis(pooled, lane % LOW * SUBLANES, axis=1, mode="promise_in_bounds")
    row = lane % bands_total // LOW * 2
    sums = jnp.sum(jnp.where(sublane == row, pooled, 0.0), axis=0, keepdims=True)
    counts = jnp.sum(jnp.where(sublane == row + 1, pooled, 0.0), axis=0, keepdims=True)
    table = target_ref[...] - sums / (counts + 1.0)
    table = jnp.where(lane < bands_total, table, 0.0)
    for k in range(code_ref.shape[1] // LANES):
        here = slice(k * LANES, (k + 1) * LANES)
        applied = jnp.take_along_axis(table, code_ref[:, here], axis=1, mode="promise_in_bounds")
        out_ref[:, here] = smoothed_ref[:, here] + applied


def shards(ensemble, band_index, region_cells, target_means):
    region_count = lax.axis_size("region")
    _, rows, width = ensemble.shape
    bands_total = target_means.shape[1]
    inner_pairs = [(i, i ^ 1) for i in range(region_count)]
    outer_pairs = [(i, ((i + 1) ^ 1) - 1) for i in range(1, region_count - 1)]
    field, band = ensemble[0], band_index[0]
    vmem = pl.BlockSpec(memory_space=pltpu.VMEM)

    def shape(count, columns, kind=jnp.float32):
        return jax.ShapeDtypeStruct((count, columns), kind)

    tile, block = shape(rows, width), shape(SUBLANES, LANES)

    def call(kernel, name, outs, ins, flops, **more):
        return pl.pallas_call(
            functools.partial(kernel, bands_total),
            out_shape=outs,
            in_specs=ins,
            out_specs=jax.tree.map(lambda _: vmem, outs),
            compiler_params=pltpu.CompilerParams(vmem_limit_bytes=16 * 2**20),
            cost_estimate=pl.CostEstimate(flops=flops, bytes_accessed=2**20, transcendentals=0),
            name=name,
            **more,
        )

    inner_sent, field, band, target = call(
        load_kernel, "load", (shape(2, width), tile, shape(rows, width, jnp.int32), shape(1, 2 * bands_total)),
        [pl.BlockSpec(memory_space=pltpu.HBM)] * 3, 10**6,
        scratch_shapes=[pltpu.VMEM((1, bands_total), jnp.float32), pltpu.SemaphoreType.DMA((3,))],
    )(*[pltpu.with_memory_space_constraint(a, pltpu.HBM) for a in (field, band, target_means)])
    inner_got = lax.ppermute(inner_sent, "region", inner_pairs)
    payload = shape(4, width + 2 * LANES)
    base, code, edge_code, sent, prepared = call(
        prepare_kernel, "prepare",
        (tile, shape(rows, width, jnp.int32), shape(rows, width // 4), shape(4, width), block),
        [pl.BlockSpec(memory_space=pltpu.SMEM), vmem, vmem], 4 * 10**9,
    )(region_cells, field, band)
    added, sent = call(
        inner_kernel, "inner", (shape(rows, width // 4), payload), [vmem] * 4, 10**9
    )(inner_got, edge_code, prepared, sent)
    got = lax.ppermute(sent, "region", outer_pairs)
    members = lax.axis_size("member")
    blocks_out = jax.ShapeDtypeStruct((2 * members, SUBLANES, LANES), jnp.float32)
    smoothed, blocks = call(outer_kernel, "outer", (tile, blocks_out), [vmem] * 4, 10**9)(
        got, sent, base, added
    )
    groups = [[2 * members * k + i for i in range(2 * members)] for k in range(region_count // 2)]
    pieces = lax.all_to_all(blocks, ("region", "member"), 0, 0, axis_index_groups=groups, tiled=True)
    out = call(apply_kernel, "apply", tile, [vmem] * 4, 10**9)(pieces, target, code, smoothed)
    return out[None]


def solution(mesh):
    placed = (
        P("member", "region", None),
        P("member", "region", None),
        P("region"),
        P("region", None),
    )
    return jax.shard_map(
        shards, mesh=mesh, in_specs=placed, out_specs=P("member", "region", None), check_vma=False
    )
```

time: 109 us -> 33.4 us (0.31)
  the two profiles are of different devices: /device:TPU:190 before, /device:TPU:188 now
where the time goes in v3:
time: 33.4 us; the launch traced here: 33.2 us
  blocking collectives  16.2 us (49%)
  starting transfers between devices  5.55 us (17%)
  waiting for transfers between devices  5.4 us (16%)
  Pallas kernels  5.36 us (16%)
  between operations  0.69 us (2%)
    all_to_all x1, blocking collectives, shards(): lax.all_to_all(blocks, ('region', 'member'), 0, 0, axis_index_groups=grou...  16.2 us
    ppermute x1, waiting for transfers between devices, shards(): got = lax.ppermute(sent, 'region', outer_pairs)  4.45 us
    ppermute x1, starting transfers between devices, shards(): inner_got = lax.ppermute(inner_sent, 'region', inner_pairs)  3.11 us
    ppermute x1, starting transfers between devices, shards(): got = lax.ppermute(sent, 'region', outer_pairs)  2.45 us
    pallas_call x1, Pallas kernels, shards(): call(prepare_kernel, 'prepare', (tile, shape(rows, width, jnp.int32), sha...  1.45 us
    pallas_call x1, Pallas kernels, shards(): call(apply_kernel, 'apply', tile, [vmem] * 4, 10 ** 9)  1.24 us
    pallas_call x1, Pallas kernels, shards(): call(load_kernel, 'load', (shape(2, width), tile, shape(rows, width, jnp....  1.12 us
    ppermute x1, waiting for transfers between devices, shards(): inner_got = lax.ppermute(inner_sent, 'region', inner_pairs)  0.95 us
  transfers between devices with their start and end apart: 2, of which 2 were waited for; matrix products, arithmetic and copies ran while one was open for 0% of the time, Pallas kernels for 4%

profile of v3, /device:TPU:188, one launch (start us, length us, event | category | flops | bytes accessed | tf_op | source)
XLA Modules:
  0.0 33.2 jit_solution(14275033021508575385)
XLA Ops:
  0.0 1.1 %load.1 = (f32[2,8192]{1,0:T(2,128)S(1)}, f32[8,8192]{1,0:T(8,128)S(1)}, s32[8,8192]{1,0:T(8,128)S(1)}, f32[1,128]{1,0:T(1,128)S(1)}) custom-call(f32[8,8192]{1,0:T(8,128)} %bitcast.3, s32[8,8192]{1,0:T(8,128)} %bitcast.4, f32[1,64]{1,0:T(1,128)} %target_hbm.1), custom_call_target="tpu_custom_call" | custom-call | flops 1000000 | bytes 1048576 | tf_op jit(solution)/shard_map/load/pallas_call | solution.py:246
  1.1 3.1 %collective-permute-start = (f32[2,8192]{1,0:T(2,128)S(1)}, f32[2,8192]{1,0:T(2,128)S(1)}, u32[]{:S(2)}, u32[]{:S(2)}) collective-permute-start(f32[2,8192]{1,0:T(2,128)S(1)} %get-tuple-element.18), channel_id=1, source_target_pairs={{0,4},{4,0},{8,12},{12,8},{16,20},{20,16},{24,28},{28,24},{32,36},... | collective-permute-start | bytes 196616 | tf_op jit(solution)/shard_map/ppermute | solution.py:251
  4.9 1.4 %prepare.1 = (f32[8,8192]{1,0:T(8,128)S(1)}, s32[8,8192]{1,0:T(8,128)S(1)}, f32[8,2048]{1,0:T(8,128)S(1)}, f32[4,8192]{1,0:T(4,128)S(1)}, f32[8,128]{1,0:T(8,128)S(1)}) custom-call(s32[1]{0:T(128)S(6)} %copy.5.cells_ref, f32[8,8192]{1,0:T(8,128)S(1)} %get-tuple-element.19.center_ref, s32[8,8192]{1,0:T(8,128)S(1)} %get-tuple-element.20.band_ref), custom_call_target="tpu_custom_call" | custom-call | flops 4000000000 | bytes 1048576 | tf_op jit(solution)/shard_map/prepare/pallas_call | solution.py:253
  6.3 0.9 %collective-permute-done.got_ref = f32[2,8192]{1,0:T(2,128)S(1)} collective-permute-done((f32[2,8192]{1,0:T(2,128)S(1)}, f32[2,8192]{1,0:T(2,128)S(1)}, u32[]{:S(2)}, u32[]{:S(2)}) %collective-permute-start) | collective-permute-done | bytes 65568 | tf_op jit(solution)/shard_map/ppermute | solution.py:251
  7.3 0.6 %inner.1 = (f32[8,2048]{1,0:T(8,128)S(1)}, f32[4,8448]{1,0:T(4,128)S(1)}) custom-call(f32[2,8192]{1,0:T(2,128)S(1)} %collective-permute-done.got_ref, f32[8,2048]{1,0:T(8,128)S(1)} %get-tuple-element.21.code_ref, f32[8,128]{1,0:T(8,128)S(1)} %get-tuple-element.22.prepared_ref, f32[4,8192]{1,0:T(4,128)S(1)} %get-tuple-element.23.edge_ref), custom_call_target="tpu_custom_call" | custom-call | flops 1000000000 | bytes 1048576 | tf_op jit(solution)/shard_map/inner/pallas_call | solution.py:258
  7.9 2.4 %collective-permute-start.1 = (f32[4,8448]{1,0:T(4,128)S(1)}, f32[4,8448]{1,0:T(4,128)S(1)}, u32[]{:S(2)}, u32[]{:S(2)}) collective-permute-start(f32[4,8448]{1,0:T(4,128)S(1)} %get-tuple-element.24.sent_ref), channel_id=1, source_target_pairs={{4,8},{8,4},{12,16},{16,12},{20,24},{24,20},{28,32},{32,28},{36,40... | collective-permute-start | bytes 405512 | tf_op jit(solution)/shard_map/ppermute | solution.py:261
  10.4 4.4 %collective-permute-done.1.got_ref = f32[4,8448]{1,0:T(4,128)S(1)} collective-permute-done((f32[4,8448]{1,0:T(4,128)S(1)}, f32[4,8448]{1,0:T(4,128)S(1)}, u32[]{:S(2)}, u32[]{:S(2)}) %collective-permute-start.1) | collective-permute-done | bytes 135200 | tf_op jit(solution)/shard_map/ppermute | solution.py:261
  14.8 0.9 %outer.1 = (f32[8,8192]{1,0:T(8,128)S(1)}, f32[8,8,128]{2,1,0:T(8,128)S(1)}) custom-call(f32[4,8448]{1,0:T(4,128)S(1)} %collective-permute-done.1.got_ref, f32[4,8448]{1,0:T(4,128)S(1)} %get-tuple-element.24.sent_ref, f32[8,8192]{1,0:T(8,128)S(1)} %get-tuple-element.25.base_ref, f32[8,2048]{1,0:T(8,128)S(1)} %get-tuple-element.26.added_ref), custom_call_target="tpu_custom_call" | custom-call | flops 1000000000 | bytes 1048576 | tf_op jit(solution)/shard_map/outer/pallas_call | solution.py:264
  15.8 16.2 %all_to_all.5.blocks_ref = f32[8,8,128]{2,1,0:T(8,128)S(1)} all-to-all(f32[8,8,128]{2,1,0:T(8,128)S(1)} %get-tuple-element.27), channel_id=1, replica_groups={{0,1,2,3,4,5,6,7},{8,9,10,11,12,13,14,15},{16,17,18,19,20,21,22,23},{24..., dimensions={0} | all-to-all | bytes 65536 | tf_op jit(solution)/shard_map/all_to_all | solution.py:268
  32.0 1.2 %apply.1 = f32[8,8192]{1,0:T(8,128)} custom-call(f32[8,8,128]{2,1,0:T(8,128)S(1)} %all_to_all.5.blocks_ref, f32[1,128]{1,0:T(1,128)S(1)} %get-tuple-element.28.target_ref, s32[8,8192]{1,0:T(8,128)S(1)} %get-tuple-element.29.code_ref, f32[8,8192]{1,0:T(8,128)S(1)} %get-tuple-element.30.smoothed_ref), custom_call_target="tpu_custom_call" | custom-call | flops 1000000000 | bytes 1048576 | tf_op jit(solution)/shard_map/apply/pallas_call | solution.py:269
Async XLA Ops:
  1.1 6.2 %collective-permute-start = (f32[2,8192]{1,0:T(2,128)S(1)}, f32[2,8192]{1,0:T(2,128)S(1)}, u32[]{:S(2)}, u32[]{:S(2)}) collective-permute-start(f32[2,8192]{1,0:T(2,128)S(1)} %get-tuple-element.18), channel_id=1, source_target_pairs={{0,4},{4,0},{8,12},{12,8},{16,20},{20,16},{24,28},{28,24},{32,36},... | collective-permute-start | bytes 196616 | tf_op jit(solution)/shard_map/ppermute | solution.py:251
  7.9 6.9 %collective-permute-start.1 = (f32[4,8448]{1,0:T(4,128)S(1)}, f32[4,8448]{1,0:T(4,128)S(1)}, u32[]{:S(2)}, u32[]{:S(2)}) collective-permute-start(f32[4,8448]{1,0:T(4,128)S(1)} %get-tuple-element.24.sent_ref), channel_id=1, source_target_pairs={{4,8},{8,4},{12,16},{16,12},{20,24},{24,20},{28,32},{32,28},{36,40... | collective-permute-start | bytes 405512 | tf_op jit(solution)/shard_map/ppermute | solution.py:261

commit v4 on v3

--- a/solution.py
+++ b/solution.py
@@ -25,14 +25,15 @@
     width = field.shape[1]
     lane = iota(field.shape, 1)
 
-    def shifted(values, by, edge, turn):
-        moved = pltpu.roll(values, by, 1)
-        return jnp.where(lane == edge, pltpu.roll(moved, turn, 0), moved) if kept else moved
-
-    for _ in range(2):
-        field = field + shifted(field, 1, 0, kept)
-        field = field + shifted(field, width - 1, width - 1, SUBLANES - kept)
-    return field
+    def shifted(by):
+        moved = pltpu.roll(field, by % width, 1)
+        if not kept:
+            return moved
+        crossed = lane < by if by > 0 else lane >= width + by
+        return jnp.where(crossed, pltpu.roll(moved, kept if by > 0 else SUBLANES - kept, 0), moved)
+
+    near, far = shifted(1) + shifted(-1), shifted(2) + shifted(-2)
+    return far + 4.0 * near + 6.0 * field
 
 
 def bf16_terms(values):
@@ -84,11 +85,10 @@
     return total
 
 
-def load_kernel(bands_total, field_hbm, band_hbm, target_hbm, inner_ref, field_ref, band_ref, target_ref, target, sems):
+def load_kernel(_, field_hbm, band_hbm, inner_ref, field_ref, band_ref, sems):
     copies = [
         pltpu.make_async_copy(field_hbm, field_ref, sems.at[0]),
         pltpu.make_async_copy(band_hbm, band_ref, sems.at[1]),
-        pltpu.make_async_copy(target_hbm, target, sems.at[2]),
     ]
     for copy in copies:
         copy.start()
@@ -97,12 +97,11 @@
     rows = field_ref.shape[0]
     inner_ref[...] = jnp.where(even, field_ref[rows - 2 :, :], field_ref[:2, :])
     copies[1].wait()
-    copies[2].wait()
-    target_ref[:, :bands_total] = target[...]
-    target_ref[:, bands_total:] = target[...]
-
-
-def prepare_kernel(bands_total, cells_ref, center_ref, band_ref, base_ref, code_ref, edge_code_ref, sent_ref, stats_ref):
+
+
+def prepare_kernel(bands_total, cells_ref, center_ref, band_ref, target_hbm, base_ref, code_ref, edge_code_ref, sent_ref, stats_ref, target_ref, target, sem):
+    copy = pltpu.make_async_copy(target_hbm, target, sem)
+    copy.start()
     at_north, at_south, even = rank_flags()
     center = center_ref[...]
     rows, width = center.shape
@@ -134,6 +133,9 @@
     sent_ref[0:2, :] = jnp.where(even, center[:2], center[rows - 2 :])
     sent_ref[2:4, :] = jnp.where(even, code[:2], code[rows - 2 :])
     (stats_ref[...],) = band_blocks(bands_total, code, base, [(None, True)])
+    copy.wait()
+    target_ref[:, :bands_total] = target[...]
+    target_ref[:, bands_total:] = target[...]
 
 
 def inner_kernel(bands_total, got_ref, code_ref, prepared_ref, edge_ref, added_ref, sent_ref):
@@ -202,10 +204,13 @@
 
 def apply_kernel(bands_total, blocks_ref, target_ref, code_ref, smoothed_ref, out_ref):
     pooled = jnp.sum(blocks_ref[...], axis=0)
-    for shift in (1, 2, 4):
-        pooled = pooled + pltpu.roll(pooled, LANES - shift, 1)
     sublane, lane = iota(pooled.shape, 0), iota(pooled.shape, 1)
-    pooled = jnp.take_along_axis(pooled, lane % LOW * SUBLANES, axis=1, mode="promise_in_bounds")
+    parts = [
+        jnp.take_along_axis(pooled, lane % LOW * SUBLANES + k, axis=1, mode="promise_in_bounds") for k in range(SUBLANES)
+    ]
+    while len(parts) > 1:
+        parts = [a + b for a, b in zip(parts[::2], parts[1::2])]
+    (pooled,) = parts
     row = lane % bands_total // LOW * 2
     sums = jnp.sum(jnp.where(sublane == row, pooled, 0.0), axis=0, keepdims=True)
     counts = jnp.sum(jnp.where(sublane == row + 1, pooled, 0.0), axis=0, keepdims=True)
@@ -243,18 +248,18 @@
             **more,
         )
 
-    inner_sent, field, band, target = call(
-        load_kernel, "load", (shape(2, width), tile, shape(rows, width, jnp.int32), shape(1, 2 * bands_total)),
-        [pl.BlockSpec(memory_space=pltpu.HBM)] * 3, 10**6,
-        scratch_shapes=[pltpu.VMEM((1, bands_total), jnp.float32), pltpu.SemaphoreType.DMA((3,))],
-    )(*[pltpu.with_memory_space_constraint(a, pltpu.HBM) for a in (field, band, target_means)])
+    inner_sent, field, band = call(
+        load_kernel, "load", (shape(2, width), tile, shape(rows, width, jnp.int32)),
+        [pl.BlockSpec(memory_space=pltpu.HBM)] * 2, 10**6, scratch_shapes=[pltpu.SemaphoreType.DMA((2,))],
+    )(*[pltpu.with_memory_space_constraint(a, pltpu.HBM) for a in (field, band)])
     inner_got = lax.ppermute(inner_sent, "region", inner_pairs)
     payload = shape(4, width + 2 * LANES)
-    base, code, edge_code, sent, prepared = call(
+    base, code, edge_code, sent, prepared, target = call(
         prepare_kernel, "prepare",
-        (tile, shape(rows, width, jnp.int32), shape(rows, width // 4), shape(4, width), block),
-        [pl.BlockSpec(memory_space=pltpu.SMEM), vmem, vmem], 4 * 10**9,
-    )(region_cells, field, band)
+        (tile, shape(rows, width, jnp.int32), shape(rows, width // 4), shape(4, width), block, shape(1, 2 * bands_total)),
+        [pl.BlockSpec(memory_space=pltpu.SMEM), vmem, vmem, pl.BlockSpec(memory_space=pltpu.HBM)], 4 * 10**9,
+        scratch_shapes=[pltpu.VMEM((1, bands_total), jnp.float32), pltpu.SemaphoreType.DMA],
+    )(region_cells, field, band, pltpu.with_memory_space_constraint(target_means, pltpu.HBM))
     added, sent = call(
         inner_kernel, "inner", (shape(rows, width // 4), payload), [vmem] * 4, 10**9
     )(inner_got, edge_code, prepared, sent)

time: 33.4 us -> 32.6 us (0.976)
  Pallas kernels: 5.36 us -> 4.68 us
    pallas_call x1, Pallas kernels: 0.94 us -> 0.59 us  [shards(): call(outer_kernel, 'outer', (tile, blocks_out), [vmem] * 4, 10 ** 9)]
  transfers between devices with their start and end apart: 2 -> 2, of which waited for: 2 -> 2; matrix products, arithmetic and copies ran while one was open for 0% -> 0% of each run, Pallas kernels for 4% -> 5%
where the time goes in v4:
time: 32.6 us; the launch traced here: 32.4 us
  blocking collectives  16.2 us (50%)
  starting transfers between devices  5.55 us (17%)
  waiting for transfers between devices  5.25 us (16%)
  Pallas kernels  4.68 us (14%)
  between operations  0.69 us (2%)
    all_to_all x1, blocking collectives, shards(): lax.all_to_all(blocks, ('region', 'member'), 0, 0, axis_index_groups=grou...  16.2 us
    ppermute x1, waiting for transfers between devices, shards(): got = lax.ppermute(sent, 'region', outer_pairs)  4.45 us
    ppermute x1, starting transfers between devices, shards(): inner_got = lax.ppermute(inner_sent, 'region', inner_pairs)  3.11 us
    ppermute x1, starting transfers between devices, shards(): got = lax.ppermute(sent, 'region', outer_pairs)  2.45 us
    pallas_call x1, Pallas kernels, shards(): call(prepare_kernel, 'prepare', (tile, shape(rows, width, jnp.int32), sha...  1.59 us
    pallas_call x1, Pallas kernels, shards(): call(apply_kernel, 'apply', tile, [vmem] * 4, 10 ** 9)  1.06 us
    pallas_call x1, Pallas kernels, shards(): call(load_kernel, 'load', (shape(2, width), tile, shape(rows, width, jnp....  1.04 us
    ppermute x1, waiting for transfers between devices, shards(): inner_got = lax.ppermute(inner_sent, 'region', inner_pairs)  0.8 us
  transfers between devices with their start and end apart: 2, of which 2 were waited for; matrix products, arithmetic and copies ran while one was open for 0% of the time, Pallas kernels for 5%

profile of v4, /device:TPU:188, one launch (start us, length us, event | category | flops | bytes accessed | tf_op | source)
XLA Modules:
  0.0 32.4 jit_solution(13726399391262890030)
XLA Ops:
  0.0 1.0 %load.1 = (f32[2,8192]{1,0:T(2,128)S(1)}, f32[8,8192]{1,0:T(8,128)S(1)}, s32[8,8192]{1,0:T(8,128)S(1)}) custom-call(f32[8,8192]{1,0:T(8,128)} %bitcast.3, s32[8,8192]{1,0:T(8,128)} %bitcast.4), custom_call_target="tpu_custom_call" | custom-call | flops 1000000 | bytes 1048576 | tf_op jit(solution)/shard_map/load/pallas_call | solution.py:251
  1.1 3.1 %collective-permute-start = (f32[2,8192]{1,0:T(2,128)S(1)}, f32[2,8192]{1,0:T(2,128)S(1)}, u32[]{:S(2)}, u32[]{:S(2)}) collective-permute-start(f32[2,8192]{1,0:T(2,128)S(1)} %get-tuple-element.18), channel_id=1, source_target_pairs={{0,4},{4,0},{8,12},{12,8},{16,20},{20,16},{24,28},{28,24},{32,36},... | collective-permute-start | bytes 196616 | tf_op jit(solution)/shard_map/ppermute | solution.py:255
  4.8 1.6 %prepare.1 = (f32[8,8192]{1,0:T(8,128)S(1)}, s32[8,8192]{1,0:T(8,128)S(1)}, f32[8,2048]{1,0:T(8,128)S(1)}, f32[4,8192]{1,0:T(4,128)S(1)}, f32[8,128]{1,0:T(8,128)S(1)}, /*index=5*/f32[1,128]{1,0:T(1,128)S(1)}) custom-call(s32[1]{0:T(128)S(6)} %copy.5.cells_ref, f32[8,8192]{1,0:T(8,128)S(1)} %get-tuple-element.19.center_ref, ...), custom_call_target="tpu_custom_call" | custom-call | flops 4000000000 | bytes 1048576 | tf_op jit(solution)/shard_map/prepare/pallas_call | solution.py:257
  6.4 0.8 %collective-permute-done.got_ref = f32[2,8192]{1,0:T(2,128)S(1)} collective-permute-done((f32[2,8192]{1,0:T(2,128)S(1)}, f32[2,8192]{1,0:T(2,128)S(1)}, u32[]{:S(2)}, u32[]{:S(2)}) %collective-permute-start) | collective-permute-done | bytes 65568 | tf_op jit(solution)/shard_map/ppermute | solution.py:255
  7.2 0.4 %inner.1 = (f32[8,2048]{1,0:T(8,128)S(1)}, f32[4,8448]{1,0:T(4,128)S(1)}) custom-call(f32[2,8192]{1,0:T(2,128)S(1)} %collective-permute-done.got_ref, f32[8,2048]{1,0:T(8,128)S(1)} %get-tuple-element.21.code_ref, f32[8,128]{1,0:T(8,128)S(1)} %get-tuple-element.22.prepared_ref, f32[4,8192]{1,0:T(4,128)S(1)} %get-tuple-element.23.edge_ref), custom_call_target="tpu_custom_call" | custom-call | flops 1000000000 | bytes 1048576 | tf_op jit(solution)/shard_map/inner/pallas_call | solution.py:263
  7.6 2.4 %collective-permute-start.1 = (f32[4,8448]{1,0:T(4,128)S(1)}, f32[4,8448]{1,0:T(4,128)S(1)}, u32[]{:S(2)}, u32[]{:S(2)}) collective-permute-start(f32[4,8448]{1,0:T(4,128)S(1)} %get-tuple-element.24.sent_ref), channel_id=1, source_target_pairs={{4,8},{8,4},{12,16},{16,12},{20,24},{24,20},{28,32},{32,28},{36,40... | collective-permute-start | bytes 405512 | tf_op jit(solution)/shard_map/ppermute | solution.py:266
  10.1 4.5 %collective-permute-done.1.got_ref = f32[4,8448]{1,0:T(4,128)S(1)} collective-permute-done((f32[4,8448]{1,0:T(4,128)S(1)}, f32[4,8448]{1,0:T(4,128)S(1)}, u32[]{:S(2)}, u32[]{:S(2)}) %collective-permute-start.1) | collective-permute-done | bytes 135200 | tf_op jit(solution)/shard_map/ppermute | solution.py:266
  14.5 0.6 %outer.1 = (f32[8,8192]{1,0:T(8,128)S(1)}, f32[8,8,128]{2,1,0:T(8,128)S(1)}) custom-call(f32[4,8448]{1,0:T(4,128)S(1)} %collective-permute-done.1.got_ref, f32[4,8448]{1,0:T(4,128)S(1)} %get-tuple-element.24.sent_ref, f32[8,8192]{1,0:T(8,128)S(1)} %get-tuple-element.25.base_ref, f32[8,2048]{1,0:T(8,128)S(1)} %get-tuple-element.26.added_ref), custom_call_target="tpu_custom_call" | custom-call | flops 1000000000 | bytes 1048576 | tf_op jit(solution)/shard_map/outer/pallas_call | solution.py:269
  15.1 16.2 %all_to_all.5.blocks_ref = f32[8,8,128]{2,1,0:T(8,128)S(1)} all-to-all(f32[8,8,128]{2,1,0:T(8,128)S(1)} %get-tuple-element.27), channel_id=1, replica_groups={{0,1,2,3,4,5,6,7},{8,9,10,11,12,13,14,15},{16,17,18,19,20,21,22,23},{24..., dimensions={0} | all-to-all | bytes 65536 | tf_op jit(solution)/shard_map/all_to_all | solution.py:273
  31.3 1.1 %apply.1 = f32[8,8192]{1,0:T(8,128)} custom-call(f32[8,8,128]{2,1,0:T(8,128)S(1)} %all_to_all.5.blocks_ref, f32[1,128]{1,0:T(1,128)S(1)} %get-tuple-element.28.target_ref, s32[8,8192]{1,0:T(8,128)S(1)} %get-tuple-element.29.code_ref, f32[8,8192]{1,0:T(8,128)S(1)} %get-tuple-element.30.smoothed_ref), custom_call_target="tpu_custom_call" | custom-call | flops 1000000000 | bytes 1048576 | tf_op jit(solution)/shard_map/apply/pallas_call | solution.py:274
Async XLA Ops:
  1.1 6.2 %collective-permute-start = (f32[2,8192]{1,0:T(2,128)S(1)}, f32[2,8192]{1,0:T(2,128)S(1)}, u32[]{:S(2)}, u32[]{:S(2)}) collective-permute-start(f32[2,8192]{1,0:T(2,128)S(1)} %get-tuple-element.18), channel_id=1, source_target_pairs={{0,4},{4,0},{8,12},{12,8},{16,20},{20,16},{24,28},{28,24},{32,36},... | collective-permute-start | bytes 196616 | tf_op jit(solution)/shard_map/ppermute | solution.py:255
  7.6 6.9 %collective-permute-start.1 = (f32[4,8448]{1,0:T(4,128)S(1)}, f32[4,8448]{1,0:T(4,128)S(1)}, u32[]{:S(2)}, u32[]{:S(2)}) collective-permute-start(f32[4,8448]{1,0:T(4,128)S(1)} %get-tuple-element.24.sent_ref), channel_id=1, source_target_pairs={{4,8},{8,4},{12,16},{16,12},{20,24},{24,20},{28,32},{32,28},{36,40... | collective-permute-start | bytes 405512 | tf_op jit(solution)/shard_map/ppermute | solution.py:266

commit v5 on v4

--- a/solution.py
+++ b/solution.py
@@ -23,14 +23,17 @@
 
 def smooth_along(field, kept):
     width = field.shape[1]
-    lane = iota(field.shape, 1)
+    lane = iota((SUBLANES, LANES), 1)
 
     def shifted(by):
         moved = pltpu.roll(field, by % width, 1)
         if not kept:
             return moved
-        crossed = lane < by if by > 0 else lane >= width + by
-        return jnp.where(crossed, pltpu.roll(moved, kept if by > 0 else SUBLANES - kept, 0), moved)
+        edge = moved[:, :LANES] if by > 0 else moved[:, width - LANES :]
+        crossed = lane < by if by > 0 else lane >= LANES + by
+        edge = jnp.where(crossed, pltpu.roll(edge, kept if by > 0 else SUBLANES - kept, 0), edge)
+        pieces = [edge, moved[:, LANES:]] if by > 0 else [moved[:, : width - LANES], edge]
+        return jnp.concatenate(pieces, axis=1)
 
     near, far = shifted(1) + shifted(-1), shifted(2) + shifted(-2)
     return far + 4.0 * near + 6.0 * field
@@ -159,9 +162,9 @@
     sent_ref[:, width + LANES :] = block[4:]
 
 
-def outer_kernel(bands_total, got_ref, sent_ref, base_ref, added_ref, smoothed_ref, blocks_ref):
+def outer_kernel(bands_total, got_ref, sent_ref, outer_added_ref, blocks_ref):
     at_north, at_south, even = rank_flags()
-    rows, width = base_ref.shape
+    width = got_ref.shape[1] - 2 * LANES
     half = width // 2
     shape = (SUBLANES, half)
     low = iota(shape, 0) < SUBLANES // 2
@@ -189,20 +192,10 @@
     count = blocks_ref.shape[0]
     for k in range(count):
         blocks_ref[k] = own + jnp.where((k < count // 2) == even, cross, 0.0)
-    piece = width // 4
-    row = iota((rows, piece), 0)
-    inner_start = jnp.where(even, rows - 2, 0)
-    outer_start = jnp.where(even, 0, rows - 2)
-    inner_row, outer_row = row // 2 == inner_start // 2, row // 2 == outer_start // 2
-    for q in range(4):
-        here = slice(q * piece, (q + 1) * piece)
-        there = slice(q % 2 * piece, (q % 2 + 1) * piece)
-        inner = pltpu.roll(added_ref[...], inner_start + (SUBLANES - 2 * q), 0)
-        outer = pltpu.roll(added[:, there], outer_start + (SUBLANES - q // 2 * 4), 0)
-        smoothed_ref[:, here] = base_ref[:, here] + jnp.where(inner_row, inner, jnp.where(outer_row, outer, 0.0))
-
-
-def apply_kernel(bands_total, blocks_ref, target_ref, code_ref, smoothed_ref, out_ref):
+    outer_added_ref[...] = added
+
+
+def apply_kernel(bands_total, blocks_ref, target_ref, code_ref, base_ref, added_ref, outer_ref, out_hbm, out, sems):
     pooled = jnp.sum(blocks_ref[...], axis=0)
     sublane, lane = iota(pooled.shape, 0), iota(pooled.shape, 1)
     parts = [
@@ -216,10 +209,28 @@
     counts = jnp.sum(jnp.where(sublane == row + 1, pooled, 0.0), axis=0, keepdims=True)
     table = target_ref[...] - sums / (counts + 1.0)
     table = jnp.where(lane < bands_total, table, 0.0)
-    for k in range(code_ref.shape[1] // LANES):
-        here = slice(k * LANES, (k + 1) * LANES)
-        applied = jnp.take_along_axis(table, code_ref[:, here], axis=1, mode="promise_in_bounds")
-        out_ref[:, here] = smoothed_ref[:, here] + applied
+    _, _, even = rank_flags()
+    rows, width = base_ref.shape
+    inner_start = jnp.where(even, rows - 2, 0)
+    outer_start = jnp.where(even, 0, rows - 2)
+    inner_row, outer_row = sublane // 2 == inner_start // 2, sublane // 2 == outer_start // 2
+    piece = width // 4
+    copies = []
+    for q in range(4):
+        for k in range(piece // LANES):
+            there = slice(k * LANES, (k + 1) * LANES)
+            far = slice(q % 2 * piece + k * LANES, q % 2 * piece + (k + 1) * LANES)
+            here = slice(q * piece + k * LANES, q * piece + (k + 1) * LANES)
+            inner = pltpu.roll(added_ref[:, there], inner_start + (SUBLANES - 2 * q), 0)
+            outer = pltpu.roll(outer_ref[:, far], outer_start + (SUBLANES - q // 2 * 4), 0)
+            smoothed = base_ref[:, here] + jnp.where(inner_row, inner, jnp.where(outer_row, outer, 0.0))
+            applied = jnp.take_along_axis(table, code_ref[:, here], axis=1, mode="promise_in_bounds")
+            out[:, here] = smoothed + applied
+        whole = slice(q * piece, (q + 1) * piece)
+        copies.append(pltpu.make_async_copy(out.at[:, whole], out_hbm.at[:, whole], sems.at[q]))
+        copies[-1].start()
+    for copy in copies:
+        copy.wait()
 
 
 def shards(ensemble, band_index, region_cells, target_means):
@@ -236,12 +247,12 @@
 
     tile, block = shape(rows, width), shape(SUBLANES, LANES)
 
-    def call(kernel, name, outs, ins, flops, **more):
+    def call(kernel, name, outs, ins, flops, out_space=vmem, **more):
         return pl.pallas_call(
             functools.partial(kernel, bands_total),
             out_shape=outs,
             in_specs=ins,
-            out_specs=jax.tree.map(lambda _: vmem, outs),
+            out_specs=jax.tree.map(lambda _: out_space, outs),
             compiler_params=pltpu.CompilerParams(vmem_limit_bytes=16 * 2**20),
             cost_estimate=pl.CostEstimate(flops=flops, bytes_accessed=2**20, transcendentals=0),
             name=name,
@@ -266,12 +277,17 @@
     got = lax.ppermute(sent, "region", outer_pairs)
     members = lax.axis_size("member")
     blocks_out = jax.ShapeDtypeStruct((2 * members, SUBLANES, LANES), jnp.float32)
-    smoothed, blocks = call(outer_kernel, "outer", (tile, blocks_out), [vmem] * 4, 10**9)(
-        got, sent, base, added
+    outer_added, blocks = call(outer_kernel, "outer", (shape(rows, width // 2), blocks_out), [vmem] * 2, 10**9)(
+        got, sent
     )
     groups = [[2 * members * k + i for i in range(2 * members)] for k in range(region_count // 2)]
     pieces = lax.all_to_all(blocks, ("region", "member"), 0, 0, axis_index_groups=groups, tiled=True)
-    out = call(apply_kernel, "apply", tile, [vmem] * 4, 10**9)(pieces, target, code, smoothed)
+    out = call(
+        apply_kernel, "apply", tile, [vmem] * 6, 10**9, pl.BlockSpec(memory_space=pltpu.HBM),
+        scratch_shapes=[pltpu.VMEM((rows, width), jnp.float32), pltpu.SemaphoreType.DMA((4,))],
+    )(
+        pieces, target, code, base, added, outer_added
+    )
     return out[None]
 
 

time: 32.6 us -> 32.5 us (level)
  no operation moved by 1% of the time
where the time goes in v5:
time: 32.5 us; the launch traced here: 32.3 us
  blocking collectives  16.2 us (50%)
  starting transfers between devices  5.55 us (17%)
  waiting for transfers between devices  5.25 us (16%)
  Pallas kernels  4.59 us (14%)
  between operations  0.69 us (2%)
    all_to_all x1, blocking collectives, shards(): lax.all_to_all(blocks, ('region', 'member'), 0, 0, axis_index_groups=grou...  16.2 us
    ppermute x1, waiting for transfers between devices, shards(): got = lax.ppermute(sent, 'region', outer_pairs)  4.45 us
    ppermute x1, starting transfers between devices, shards(): inner_got = lax.ppermute(inner_sent, 'region', inner_pairs)  3.11 us
    ppermute x1, starting transfers between devices, shards(): got = lax.ppermute(sent, 'region', outer_pairs)  2.45 us
    pallas_call x1, Pallas kernels, shards(): call(prepare_kernel, 'prepare', (tile, shape(rows, width, jnp.int32), sha...  1.59 us
    pallas_call x1, Pallas kernels, shards(): call(load_kernel, 'load', (shape(2, width), tile, shape(rows, width, jnp....  1.04 us
    pallas_call x1, Pallas kernels, shards(): call(apply_kernel, 'apply', tile, [vmem] * 6, 10 ** 9, pl.BlockSpec(memor...  1.02 us
    ppermute x1, waiting for transfers between devices, shards(): inner_got = lax.ppermute(inner_sent, 'region', inner_pairs)  0.8 us
  transfers between devices with their start and end apart: 2, of which 2 were waited for; matrix products, arithmetic and copies ran while one was open for 0% of the time, Pallas kernels for 5%

profile of v5, /device:TPU:188, one launch (start us, length us, event | category | flops | bytes accessed | tf_op | source)
XLA Modules:
  0.0 32.3 jit_solution(3449815139373148715)
XLA Ops:
  0.0 1.0 %load.1 = (f32[2,8192]{1,0:T(2,128)S(1)}, f32[8,8192]{1,0:T(8,128)S(1)}, s32[8,8192]{1,0:T(8,128)S(1)}) custom-call(f32[8,8192]{1,0:T(8,128)} %bitcast.3, s32[8,8192]{1,0:T(8,128)} %bitcast.4), custom_call_target="tpu_custom_call" | custom-call | flops 1000000 | bytes 1048576 | tf_op jit(solution)/shard_map/load/pallas_call | solution.py:262
  1.1 3.1 %collective-permute-start = (f32[2,8192]{1,0:T(2,128)S(1)}, f32[2,8192]{1,0:T(2,128)S(1)}, u32[]{:S(2)}, u32[]{:S(2)}) collective-permute-start(f32[2,8192]{1,0:T(2,128)S(1)} %get-tuple-element.18), channel_id=1, source_target_pairs={{0,4},{4,0},{8,12},{12,8},{16,20},{20,16},{24,28},{28,24},{32,36},... | collective-permute-start | bytes 196616 | tf_op jit(solution)/shard_map/ppermute | solution.py:266
  4.8 1.6 %prepare.1 = (f32[8,8192]{1,0:T(8,128)S(1)}, s32[8,8192]{1,0:T(8,128)S(1)}, f32[8,2048]{1,0:T(8,128)S(1)}, f32[4,8192]{1,0:T(4,128)S(1)}, f32[8,128]{1,0:T(8,128)S(1)}, /*index=5*/f32[1,128]{1,0:T(1,128)S(1)}) custom-call(s32[1]{0:T(128)S(6)} %copy.5.cells_ref, f32[8,8192]{1,0:T(8,128)S(1)} %get-tuple-element.19.center_ref, ...), custom_call_target="tpu_custom_call" | custom-call | flops 4000000000 | bytes 1048576 | tf_op jit(solution)/shard_map/prepare/pallas_call | solution.py:268
  6.4 0.8 %collective-permute-done.got_ref = f32[2,8192]{1,0:T(2,128)S(1)} collective-permute-done((f32[2,8192]{1,0:T(2,128)S(1)}, f32[2,8192]{1,0:T(2,128)S(1)}, u32[]{:S(2)}, u32[]{:S(2)}) %collective-permute-start) | collective-permute-done | bytes 65568 | tf_op jit(solution)/shard_map/ppermute | solution.py:266
  7.2 0.4 %inner.1 = (f32[8,2048]{1,0:T(8,128)S(1)}, f32[4,8448]{1,0:T(4,128)S(1)}) custom-call(f32[2,8192]{1,0:T(2,128)S(1)} %collective-permute-done.got_ref, f32[8,2048]{1,0:T(8,128)S(1)} %get-tuple-element.21.code_ref, f32[8,128]{1,0:T(8,128)S(1)} %get-tuple-element.22.prepared_ref, f32[4,8192]{1,0:T(4,128)S(1)} %get-tuple-element.23.edge_ref), custom_call_target="tpu_custom_call" | custom-call | flops 1000000000 | bytes 1048576 | tf_op jit(solution)/shard_map/inner/pallas_call | solution.py:274
  7.6 2.4 %collective-permute-start.1 = (f32[4,8448]{1,0:T(4,128)S(1)}, f32[4,8448]{1,0:T(4,128)S(1)}, u32[]{:S(2)}, u32[]{:S(2)}) collective-permute-start(f32[4,8448]{1,0:T(4,128)S(1)} %get-tuple-element.24.sent_ref), channel_id=1, source_target_pairs={{4,8},{8,4},{12,16},{16,12},{20,24},{24,20},{28,32},{32,28},{36,40... | collective-permute-start | bytes 405512 | tf_op jit(solution)/shard_map/ppermute | solution.py:277
  10.1 4.5 %collective-permute-done.1.got_ref = f32[4,8448]{1,0:T(4,128)S(1)} collective-permute-done((f32[4,8448]{1,0:T(4,128)S(1)}, f32[4,8448]{1,0:T(4,128)S(1)}, u32[]{:S(2)}, u32[]{:S(2)}) %collective-permute-start.1) | collective-permute-done | bytes 135200 | tf_op jit(solution)/shard_map/ppermute | solution.py:277
  14.5 0.5 %outer.1 = (f32[8,4096]{1,0:T(8,128)S(1)}, f32[8,8,128]{2,1,0:T(8,128)S(1)}) custom-call(f32[4,8448]{1,0:T(4,128)S(1)} %collective-permute-done.1.got_ref, f32[4,8448]{1,0:T(4,128)S(1)} %get-tuple-element.24.sent_ref), custom_call_target="tpu_custom_call" | custom-call | flops 1000000000 | bytes 1048576 | tf_op jit(solution)/shard_map/outer/pallas_call | solution.py:280
  15.1 16.2 %all_to_all.5.blocks_ref = f32[8,8,128]{2,1,0:T(8,128)S(1)} all-to-all(f32[8,8,128]{2,1,0:T(8,128)S(1)} %get-tuple-element.25), channel_id=1, replica_groups={{0,1,2,3,4,5,6,7},{8,9,10,11,12,13,14,15},{16,17,18,19,20,21,22,23},{24..., dimensions={0} | all-to-all | bytes 65536 | tf_op jit(solution)/shard_map/all_to_all | solution.py:284
  31.3 1.0 %apply.1 = f32[8,8192]{1,0:T(8,128)} custom-call(f32[8,8,128]{2,1,0:T(8,128)S(1)} %all_to_all.5.blocks_ref, f32[1,128]{1,0:T(1,128)S(1)} %get-tuple-element.26.target_ref, s32[8,8192]{1,0:T(8,128)S(1)} %get-tuple-element.27.code_ref, f32[8,8192]{1,0:T(8,128)S(1)} %get-tuple-element.28.base_ref, f32[8,2048]{1,0:T(8,128)S(1)} %get-tuple-element.29.added_ref, ...), custom_call_target="tpu_custom_call" | custom-call | flops 1000000000 | bytes 1048576 | tf_op jit(solution)/shard_map/apply/pallas_call | solution.py:285
Async XLA Ops:
  1.1 6.2 %collective-permute-start = (f32[2,8192]{1,0:T(2,128)S(1)}, f32[2,8192]{1,0:T(2,128)S(1)}, u32[]{:S(2)}, u32[]{:S(2)}) collective-permute-start(f32[2,8192]{1,0:T(2,128)S(1)} %get-tuple-element.18), channel_id=1, source_target_pairs={{0,4},{4,0},{8,12},{12,8},{16,20},{20,16},{24,28},{28,24},{32,36},... | collective-permute-start | bytes 196616 | tf_op jit(solution)/shard_map/ppermute | solution.py:266
  7.6 6.9 %collective-permute-start.1 = (f32[4,8448]{1,0:T(4,128)S(1)}, f32[4,8448]{1,0:T(4,128)S(1)}, u32[]{:S(2)}, u32[]{:S(2)}) collective-permute-start(f32[4,8448]{1,0:T(4,128)S(1)} %get-tuple-element.24.sent_ref), channel_id=1, source_target_pairs={{4,8},{8,4},{12,16},{16,12},{20,24},{24,20},{28,32},{32,28},{36,40... | collective-permute-start | bytes 405512 | tf_op jit(solution)/shard_map/ppermute | solution.py:277

commit v6 on v5

--- a/solution.py
+++ b/solution.py
@@ -46,18 +46,23 @@
     return [high, middle, rest - middle]
 
 
-def band_blocks(bands_total, code, values, groups):
+def low_columns(code):
+    lower = code - jnp.floor(code * (1.0 / LOW)) * LOW
+    lower = jnp.concatenate([lower, lower - 1.0], axis=0).astype(jnp.bfloat16)
+    zero, one = jnp.zeros((), jnp.bfloat16), jnp.ones((), jnp.bfloat16)
+    return jnp.concatenate([jnp.where(lower == b, one, zero) for b in range(0, LOW, 2)], axis=0)
+
+
+def band_blocks(bands_total, code, values, groups, right=None):
     blocks = bands_total // LOW
     upper = jnp.floor(code * (1.0 / LOW))
-    lower = code - upper * LOW
     terms = bf16_terms(values)
     terms.append(jnp.full(values.shape, 1.0, jnp.float32))
     tiles = [jnp.concatenate(terms[k : k + 2], axis=0).astype(jnp.bfloat16) for k in (0, 2)]
     upper = jnp.concatenate([upper, upper], axis=0).astype(jnp.bfloat16)
-    lower = jnp.concatenate([lower, lower - 1.0], axis=0).astype(jnp.bfloat16)
-    zero, one = jnp.zeros((), jnp.bfloat16), jnp.ones((), jnp.bfloat16)
+    zero = jnp.zeros((), jnp.bfloat16)
     left = jnp.concatenate([jnp.where(upper == a, t, zero) for a in range(blocks) for t in tiles], axis=0)
-    right = jnp.concatenate([jnp.where(lower == b, one, zero) for b in range(0, LOW, 2)], axis=0)
+    right = low_columns(code) if right is None else right
     product = lax.dot_general(left, right, (((1,), (1,)), ((), ())), preferred_element_type=jnp.float32)
     sublane, lane = iota((SUBLANES, LANES), 0), iota((SUBLANES, LANES), 1)
     made = []
@@ -102,7 +107,7 @@
     copies[1].wait()
 
 
-def prepare_kernel(bands_total, cells_ref, center_ref, band_ref, target_hbm, base_ref, code_ref, edge_code_ref, sent_ref, stats_ref, target_ref, target, sem):
+def prepare_kernel(bands_total, cells_ref, center_ref, band_ref, target_hbm, base_ref, code_ref, edge_code_ref, sent_ref, stats_ref, target_ref, columns_ref, target, sem):
     copy = pltpu.make_async_copy(target_hbm, target, sem)
     copy.start()
     at_north, at_south, even = rank_flags()
@@ -133,6 +138,7 @@
         part = pltpu.roll(code[:, q * piece : (q + 1) * piece], start + 2 * q, 0)
         packed = part if packed is None else jnp.where(iota(part.shape, 0) // 2 == q, part, packed)
     edge_code_ref[...] = packed
+    columns_ref[...] = low_columns(packed)
     sent_ref[0:2, :] = jnp.where(even, center[:2], center[rows - 2 :])
     sent_ref[2:4, :] = jnp.where(even, code[:2], code[rows - 2 :])
     (stats_ref[...],) = band_blocks(bands_total, code, base, [(None, True)])
@@ -141,7 +147,7 @@
     target_ref[:, bands_total:] = target[...]
 
 
-def inner_kernel(bands_total, got_ref, code_ref, prepared_ref, edge_ref, added_ref, sent_ref):
+def inner_kernel(bands_total, got_ref, code_ref, prepared_ref, edge_ref, columns_ref, added_ref, sent_ref):
     _, _, even = rank_flags()
     piece = got_ref.shape[1] // 4
     quarter = iota((SUBLANES, piece), 0) // 2
@@ -154,7 +160,7 @@
     added = weigh(lines[0], lines[1], even, (((1.0, 1.0), (4.0, 0.0)), ((0.0, 4.0), (1.0, 1.0))))
     added = smooth_along(added, 2)
     added_ref[...] = added
-    (block,) = band_blocks(bands_total, code_ref[...], added, [(None, False)])
+    (block,) = band_blocks(bands_total, code_ref[...], added, [(None, False)], columns_ref[...])
     block = prepared_ref[...] + block
     width = got_ref.shape[1]
     sent_ref[:, :width] = edge_ref[...]
@@ -265,15 +271,16 @@
     )(*[pltpu.with_memory_space_constraint(a, pltpu.HBM) for a in (field, band)])
     inner_got = lax.ppermute(inner_sent, "region", inner_pairs)
     payload = shape(4, width + 2 * LANES)
-    base, code, edge_code, sent, prepared, target = call(
+    base, code, edge_code, sent, prepared, target, columns = call(
         prepare_kernel, "prepare",
-        (tile, shape(rows, width, jnp.int32), shape(rows, width // 4), shape(4, width), block, shape(1, 2 * bands_total)),
+        (tile, shape(rows, width, jnp.int32), shape(rows, width // 4), shape(4, width), block, shape(1, 2 * bands_total),
+         shape(LOW * SUBLANES, width // 4, jnp.bfloat16)),
         [pl.BlockSpec(memory_space=pltpu.SMEM), vmem, vmem, pl.BlockSpec(memory_space=pltpu.HBM)], 4 * 10**9,
         scratch_shapes=[pltpu.VMEM((1, bands_total), jnp.float32), pltpu.SemaphoreType.DMA],
     )(region_cells, field, band, pltpu.with_memory_space_constraint(target_means, pltpu.HBM))
     added, sent = call(
-        inner_kernel, "inner", (shape(rows, width // 4), payload), [vmem] * 4, 10**9
-    )(inner_got, edge_code, prepared, sent)
+        inner_kernel, "inner", (shape(rows, width // 4), payload), [vmem] * 5, 10**9
+    )(inner_got, edge_code, prepared, sent, columns)
     got = lax.ppermute(sent, "region", outer_pairs)
     members = lax.axis_size("member")
     blocks_out = jax.ShapeDtypeStruct((2 * members, SUBLANES, LANES), jnp.float32)

time: 32.5 us -> 32.5 us (level)
  no operation moved by 1% of the time
where the time goes in v6:
time: 32.5 us; the launch traced here: 32.3 us
  blocking collectives  16.2 us (50%)
  starting transfers between devices  5.55 us (17%)
  waiting for transfers between devices  5.17 us (16%)
  Pallas kernels  4.68 us (14%)
  between operations  0.69 us (2%)
    all_to_all x1, blocking collectives, shards(): lax.all_to_all(blocks, ('region', 'member'), 0, 0, axis_index_groups=grou...  16.2 us
    ppermute x1, waiting for transfers between devices, shards(): got = lax.ppermute(sent, 'region', outer_pairs)  4.45 us
    ppermute x1, starting transfers between devices, shards(): inner_got = lax.ppermute(inner_sent, 'region', inner_pairs)  3.11 us
    ppermute x1, starting transfers between devices, shards(): got = lax.ppermute(sent, 'region', outer_pairs)  2.44 us
    pallas_call x1, Pallas kernels, shards(): call(prepare_kernel, 'prepare', (tile, shape(rows, width, jnp.int32), sha...  1.67 us
    pallas_call x1, Pallas kernels, shards(): call(load_kernel, 'load', (shape(2, width), tile, shape(rows, width, jnp....  1.04 us
    pallas_call x1, Pallas kernels, shards(): call(apply_kernel, 'apply', tile, [vmem] * 6, 10 ** 9, pl.BlockSpec(memor...  1.02 us
    ppermute x1, waiting for transfers between devices, shards(): inner_got = lax.ppermute(inner_sent, 'region', inner_pairs)  0.72 us
  transfers between devices with their start and end apart: 2, of which 2 were waited for; matrix products, arithmetic and copies ran while one was open for 0% of the time, Pallas kernels for 5%

profile of v6, /device:TPU:188, one launch (start us, length us, event | category | flops | bytes accessed | tf_op | source)
XLA Modules:
  0.0 32.3 jit_solution(82909006446234349)
XLA Ops:
  0.0 1.0 %load.1 = (f32[2,8192]{1,0:T(2,128)S(1)}, f32[8,8192]{1,0:T(8,128)S(1)}, s32[8,8192]{1,0:T(8,128)S(1)}) custom-call(f32[8,8192]{1,0:T(8,128)} %bitcast.3, s32[8,8192]{1,0:T(8,128)} %bitcast.4), custom_call_target="tpu_custom_call" | custom-call | flops 1000000 | bytes 1048576 | tf_op jit(solution)/shard_map/load/pallas_call | solution.py:268
  1.1 3.1 %collective-permute-start = (f32[2,8192]{1,0:T(2,128)S(1)}, f32[2,8192]{1,0:T(2,128)S(1)}, u32[]{:S(2)}, u32[]{:S(2)}) collective-permute-start(f32[2,8192]{1,0:T(2,128)S(1)} %get-tuple-element.19), channel_id=1, source_target_pairs={{0,4},{4,0},{8,12},{12,8},{16,20},{20,16},{24,28},{28,24},{32,36},... | collective-permute-start | bytes 196616 | tf_op jit(solution)/shard_map/ppermute | solution.py:272
  4.8 1.7 %prepare.1 = (f32[8,8192]{1,0:T(8,128)S(1)}, s32[8,8192]{1,0:T(8,128)S(1)}, f32[8,2048]{1,0:T(8,128)S(1)}, f32[4,8192]{1,0:T(4,128)S(1)}, f32[8,128]{1,0:T(8,128...) custom-call(s32[1]{0:T(128)S(6)} %copy.5.cells_ref, f32[8,8192]{1,0:T(8,128)S(1)} %get-tuple-element.20.center_ref, ...), custom_call_target="tpu_custom_call" | custom-call | flops 4000000000 | bytes 1048576 | tf_op jit(solution)/shard_map/prepare/pallas_call | solution.py:274
  6.5 0.7 %collective-permute-done.got_ref = f32[2,8192]{1,0:T(2,128)S(1)} collective-permute-done((f32[2,8192]{1,0:T(2,128)S(1)}, f32[2,8192]{1,0:T(2,128)S(1)}, u32[]{:S(2)}, u32[]{:S(2)}) %collective-permute-start) | collective-permute-done | bytes 65568 | tf_op jit(solution)/shard_map/ppermute | solution.py:272
  7.2 0.4 %inner.1 = (f32[8,2048]{1,0:T(8,128)S(1)}, f32[4,8448]{1,0:T(4,128)S(1)}) custom-call(f32[2,8192]{1,0:T(2,128)S(1)} %collective-permute-done.got_ref, f32[8,2048]{1,0:T(8,128)S(1)} %get-tuple-element.22.code_ref, f32[8,128]{1,0:T(8,128)S(1)} %get-tuple-element.23.prepared_ref, f32[4,8192]{1,0:T(4,128)S(1)} %get-tuple-element.24.edge_ref, ...), custom_call_target="tpu_custom_call" | custom-call | flops 1000000000 | bytes 1048576 | tf_op jit(solution)/shard_map/inner/pallas_call | solution.py:281
  7.6 2.4 %collective-permute-start.1 = (f32[4,8448]{1,0:T(4,128)S(1)}, f32[4,8448]{1,0:T(4,128)S(1)}, u32[]{:S(2)}, u32[]{:S(2)}) collective-permute-start(f32[4,8448]{1,0:T(4,128)S(1)} %get-tuple-element.26.sent_ref), channel_id=1, source_target_pairs={{4,8},{8,4},{12,16},{16,12},{20,24},{24,20},{28,32},{32,28},{36,40... | collective-permute-start | bytes 405512 | tf_op jit(solution)/shard_map/ppermute | solution.py:284
  10.1 4.5 %collective-permute-done.1.got_ref = f32[4,8448]{1,0:T(4,128)S(1)} collective-permute-done((f32[4,8448]{1,0:T(4,128)S(1)}, f32[4,8448]{1,0:T(4,128)S(1)}, u32[]{:S(2)}, u32[]{:S(2)}) %collective-permute-start.1) | collective-permute-done | bytes 135200 | tf_op jit(solution)/shard_map/ppermute | solution.py:284
  14.5 0.5 %outer.1 = (f32[8,4096]{1,0:T(8,128)S(1)}, f32[8,8,128]{2,1,0:T(8,128)S(1)}) custom-call(f32[4,8448]{1,0:T(4,128)S(1)} %collective-permute-done.1.got_ref, f32[4,8448]{1,0:T(4,128)S(1)} %get-tuple-element.26.sent_ref), custom_call_target="tpu_custom_call" | custom-call | flops 1000000000 | bytes 1048576 | tf_op jit(solution)/shard_map/outer/pallas_call | solution.py:287
  15.1 16.2 %all_to_all.5.blocks_ref = f32[8,8,128]{2,1,0:T(8,128)S(1)} all-to-all(f32[8,8,128]{2,1,0:T(8,128)S(1)} %get-tuple-element.27), channel_id=1, replica_groups={{0,1,2,3,4,5,6,7},{8,9,10,11,12,13,14,15},{16,17,18,19,20,21,22,23},{24..., dimensions={0} | all-to-all | bytes 65536 | tf_op jit(solution)/shard_map/all_to_all | solution.py:291
  31.3 1.0 %apply.1 = f32[8,8192]{1,0:T(8,128)} custom-call(f32[8,8,128]{2,1,0:T(8,128)S(1)} %all_to_all.5.blocks_ref, f32[1,128]{1,0:T(1,128)S(1)} %get-tuple-element.28.target_ref, s32[8,8192]{1,0:T(8,128)S(1)} %get-tuple-element.29.code_ref, f32[8,8192]{1,0:T(8,128)S(1)} %get-tuple-element.30.base_ref, f32[8,2048]{1,0:T(8,128)S(1)} %get-tuple-element.31.added_ref, ...), custom_call_target="tpu_custom_call" | custom-call | flops 1000000000 | bytes 1048576 | tf_op jit(solution)/shard_map/apply/pallas_call | solution.py:292
Async XLA Ops:
  1.1 6.2 %collective-permute-start = (f32[2,8192]{1,0:T(2,128)S(1)}, f32[2,8192]{1,0:T(2,128)S(1)}, u32[]{:S(2)}, u32[]{:S(2)}) collective-permute-start(f32[2,8192]{1,0:T(2,128)S(1)} %get-tuple-element.19), channel_id=1, source_target_pairs={{0,4},{4,0},{8,12},{12,8},{16,20},{20,16},{24,28},{28,24},{32,36},... | collective-permute-start | bytes 196616 | tf_op jit(solution)/shard_map/ppermute | solution.py:272
  7.6 6.9 %collective-permute-start.1 = (f32[4,8448]{1,0:T(4,128)S(1)}, f32[4,8448]{1,0:T(4,128)S(1)}, u32[]{:S(2)}, u32[]{:S(2)}) collective-permute-start(f32[4,8448]{1,0:T(4,128)S(1)} %get-tuple-element.26.sent_ref), channel_id=1, source_target_pairs={{4,8},{8,4},{12,16},{16,12},{20,24},{24,20},{28,32},{32,28},{36,40... | collective-permute-start | bytes 405512 | tf_op jit(solution)/shard_map/ppermute | solution.py:284
